TPU v7x, 256 devices: a 8x8x2 block of a 8x8x16 slice. The times are simulated.
256 devices in a mesh: groups: 2 (over z), seq: 128 (over y, x, core).
Axes of the slice: x: 8, y: 8, z: 2, core: 2. Of those that a mesh axis runs over, the one named last changes fastest.
The devices are a block of a 8x8x16 slice.
Arguments:
- queries: bfloat16 [65536, 4096], P(('groups', 'seq')), parts along dimension 0, may hold values from -13 to 13
- keys: bfloat16 [65536, 512], P(('groups', 'seq')), parts along dimension 0, may hold values from -13 to 13
- values: bfloat16 [65536, 512], P(('groups', 'seq')), parts along dimension 0, may hold values from -6 to 6
- segment_ids: int32 [65536], P(('groups', 'seq')), parts along dimension 0, may hold values from 0 to 63, as said below
Outputs:
- attended: bfloat16 [65536, 4096], P(('groups', 'seq')), parts along dimension 0
- rotated_keys: bfloat16 [65536, 512], P(('groups', 'seq')), parts along dimension 0
There are 2 independent parts, one for each index of `groups`. A program takes and returns all parts, laid end to end along the dimension named above; each array names one. Nothing has to cross between parts.
Inputs may be any that keep to these rules, and one draw needn't show every extreme that they name: `segment_ids`: never falling along the packed stream, starting at 0 and rising by one at each new rollout; each rollout covers 1 to 1792 tokens and one covers exactly 1792.
All inputs are finite; a program needn't handle non-finite values.
Results may differ from a plain program's by a relative error of at most 0.0054.
Values may be sent and summed in bfloat16 or wider, within the bound.
A program may use at most 192 MiB of HBM per device.

v0:
```python
from functools import partial

import jax
import jax.numpy as jnp
from jax import lax
from jax.sharding import Mesh
from jax.sharding import PartitionSpec as P

HD = 128
SPAN = 7
SEQ = ("seq_0", "seq_1", "seq_2")
GROUPS_SEQ = ("groups", "seq_0", "seq_1", "seq_2")


ROPE_BASE = 1000000.0
MASKED_SCORE = -1e30


def filled_with(shard, identity):
    return jax.tree.map(
        lambda a, e: jnp.broadcast_to(jnp.asarray(e, a.dtype), a.shape), shard, identity
    )


def carried_in(shard, axes, combine, identity):
    before = start = filled_with(shard, identity)
    subtotal = shard
    for axis in reversed(axes):
        length, index = (lax.axis_size(axis), lax.axis_index(axis))
        pieces = jax.tree.map(lambda part: lax.all_gather(part, axis), subtotal)
        inside, subtotal = (start, start)
        for k in range(length):
            passed = k < index
            subtotal = combine(subtotal, jax.tree.map(lambda part: part[k], pieces))
            inside = jax.tree.map(lambda new, old: jnp.where(passed, new, old), subtotal, inside)
        before = combine(inside, before)
    return before


def shifted(shard, axis, by):
    length = lax.axis_size(axis)
    pairs = [(i, i + by) for i in range(length) if 0 <= i + by < length]
    return lax.ppermute(shard, axis, pairs)


def rotate_heads(matrix, positions, head_count):
    row_count = matrix.shape[0]
    half_dim = HD // 2
    inverse_freq = ROPE_BASE ** (-(jnp.arange(half_dim, dtype=jnp.float32) * (2.0 / HD)))
    angles = positions.astype(jnp.float32)[:, None] * inverse_freq[None, :]
    cosine = jnp.cos(angles)[:, None, :]
    sine = jnp.sin(angles)[:, None, :]
    split_heads = matrix.astype(jnp.float32).reshape(row_count, head_count, HD)
    lower_half = split_heads[..., :half_dim]
    upper_half = split_heads[..., half_dim:]
    turned = jnp.concatenate(
        [lower_half * cosine - upper_half * sine, upper_half * cosine + lower_half * sine], axis=-1
    )
    return turned.reshape(row_count, head_count * HD).astype(jnp.bfloat16)


def join_runs(earlier, later):
    first_seen = jnp.where(earlier[0] >= 0, earlier[0], later[0])
    last_seen = jnp.where(later[1] >= 0, later[1], earlier[1])
    carried = (later[0] == later[1]) & (earlier[1] == later[1])
    start_seen = jnp.where(later[1] < 0, earlier[2], jnp.where(carried, earlier[2], later[2]))
    return (first_seen, last_seen, start_seen)


def attend_block(state, query_grid, key_slice, value_slice, index_slice, starts, row_index):
    row_top, row_total, weighted = state
    scores = jnp.einsum(
        "thgd,shd->thgs", query_grid, key_slice, preferred_element_type=jnp.float32
    ) * HD ** (-0.5)
    allowed = (index_slice[None, :] >= starts[:, None]) & (
        index_slice[None, :] <= row_index[:, None]
    )
    scores = jnp.where(allowed[:, None, None, :], scores, MASKED_SCORE)
    new_top = jnp.maximum(row_top, jnp.max(scores, axis=-1))
    fade = jnp.exp(row_top - new_top)
    weights = jnp.exp(scores - new_top[..., None])
    row_total = row_total * fade + jnp.sum(weights, axis=-1)
    weighted = weighted * fade[..., None] + jnp.einsum(
        "thgs,shd->thgd",
        weights.astype(jnp.bfloat16),
        value_slice,
        preferred_element_type=jnp.float32,
    )
    return (new_top, row_total, weighted)


def local(queries, keys, values, segment_ids):
    block_rows = queries.shape[0]
    query_heads = queries.shape[1] // HD
    kv_heads = keys.shape[1] // HD
    group_size = query_heads // kv_heads
    my_rank = lax.axis_index(SEQ)
    first_row = my_rank * block_rows
    row_index = first_row + jnp.arange(block_rows, dtype=jnp.int32)
    boundary = jnp.concatenate(
        [jnp.ones((1,), dtype=jnp.bool_), segment_ids[1:] != segment_ids[:-1]]
    )
    local_start = lax.cummax(jnp.where(boundary, row_index, -1), axis=0)
    summary = (segment_ids[:1], segment_ids[-1:], local_start[-1:])
    nothing = jnp.full((1,), -1, jnp.int32)
    before_runs = carried_in(summary, SEQ, join_runs, (nothing, nothing, nothing))
    starts = jnp.where(segment_ids == before_runs[1], before_runs[2], local_start)
    positions = row_index - starts
    turned_queries = rotate_heads(queries, positions, query_heads)
    turned_keys = rotate_heads(keys, positions, kv_heads)
    key_stack = turned_keys[None]
    value_stack = values[None]
    for stride_bit in range((SPAN + 1).bit_length() - 1):
        far_keys, far_values = shifted((key_stack, value_stack), SEQ, 1 << stride_bit)
        key_stack = jnp.concatenate([key_stack, far_keys], axis=0)
        value_stack = jnp.concatenate([value_stack, far_values], axis=0)
    block_count = key_stack.shape[0]
    all_keys = key_stack.reshape(block_count * block_rows, kv_heads, HD)
    all_values = value_stack.reshape(block_count * block_rows, kv_heads, HD)
    block_offset = jnp.arange(block_count, dtype=jnp.int32)
    key_index = (
        (my_rank - block_offset)[:, None] * block_rows
        + jnp.arange(block_rows, dtype=jnp.int32)[None, :]
    ).reshape(-1)
    per_step = min(block_count, max(1, 512 // block_rows))
    step_rows = per_step * block_rows
    query_grid = turned_queries.reshape(block_rows, kv_heads, group_size, HD)
    running = (
        jnp.full((block_rows, kv_heads, group_size), MASKED_SCORE, jnp.float32),
        jnp.zeros((block_rows, kv_heads, group_size), jnp.float32),
        jnp.zeros((block_rows, kv_heads, group_size, HD), jnp.float32),
    )
    for step_number in range(block_count // per_step):
        lower_row = step_number * step_rows
        index_slice = key_index[lower_row : lower_row + step_rows]
        attend_step = partial(
            attend_block,
            query_grid=query_grid,
            key_slice=all_keys[lower_row : lower_row + step_rows],
            value_slice=all_values[lower_row : lower_row + step_rows],
            index_slice=index_slice,
            starts=starts,
            row_index=row_index,
        )
        running = attend_step(running)
    row_top, row_total, weighted = running
    attended = (
        (weighted / row_total[..., None]).reshape(block_rows, query_heads * HD).astype(jnp.bfloat16)
    )
    return (attended, turned_keys)


def solution(mesh):
    split = Mesh(
        mesh.devices.reshape(mesh.shape["groups"], 8, 8, 2), ("groups", "seq_0", "seq_1", "seq_2")
    )
    return jax.shard_map(
        local,
        mesh=split,
        in_specs=(P(GROUPS_SEQ, None), P(GROUPS_SEQ, None), P(GROUPS_SEQ, None), P(GROUPS_SEQ)),
        out_specs=(P(GROUPS_SEQ, None), P(GROUPS_SEQ, None)),
        check_vma=False,
    )
```

profile of v0, /device:TPU:528, one launch (start us, length us, event | category | flops | bytes accessed | tf_op | source)
XLA Modules:
  0.0 351.7 jit_solution(12248039203219346848)
XLA Ops:
  16.7 14.4 %all-reduce.9 = (s32[8]{0:T(128)S(1)}, s32[8]{0:T(128)S(1)}, s32[8]{0:T(128)S(1)}) all-reduce(s32[8]{0:T(128)S(1)} %dynamic-update-slice.1, s32[8]{0:T(128)S(1)} %dynamic-update-slice.4, s32[8]{0:T(128)S(1)} %dynamic-update-slice.7), channel_id=3, replica_groups=mesh['groups'=2,'seq_0'=8,'seq_1'=8,'seq_2'=2] {'seq_1'}, use_global_device_ids=true, to_apply=%add.1 | all-reduce | flops 24 | bytes 192
  31.9 1.9 compare_select_fusion.22
  41.2 1.9 compare_select_fusion.27
  51.1 20.4 %all-reduce.10 = (s32[8]{0:T(128)S(1)}, s32[8]{0:T(128)S(1)}, s32[8]{0:T(128)S(1)}) all-reduce(s32[8]{0:T(128)S(1)} %dynamic-update-slice.2, s32[8]{0:T(128)S(1)} %dynamic-update-slice.5, s32[8]{0:T(128)S(1)} %dynamic-update-slice.8), channel_id=4, replica_groups=mesh['groups'=2,'seq_0'=8,'seq_1'=8,'seq_2'=2] {'seq_0'}, use_global_device_ids=true, to_apply=%add.2 | all-reduce | flops 24 | bytes 192
  128.4 2.0 collective-permute-start
  130.3 3.0 collective-permute-start.1
  133.3 2.1 convert_bitcast_fusion
  137.7 4.9 %subtract_convert_fusion = (bf16[256,32,64]{2,0,1:T(8,128)(2,1)S(1)}, bf16[256,32,64]{2,0,1:T(8,128)(2,1)S(1)}) fusion(f32[256,32,64]{2,1,0:T(8,128)S(1)} %get-tuple-element.27, f32[256,32,64]{2,1,0:T(8,128)S(1)} %get-tuple-element.26, f32[256,64]{1,0:T(8,128)S(1)} %get-tuple-element.45, f32[256,64]{1,0:T(8,128)S(1)} %get-tuple-element.44), kind=kLoop, calls=%fused_computation.39 | loop fusion | flops 4194304 | bytes 6422528 | tf_op jit(solution)/shard_map/convert.2
  144.1 3.8 %collective-permute-start.2 = (bf16[2,256,512]{2,1,0:T(8,128)(2,1)}, bf16[2,256,512]{2,1,0:T(8,128)(2,1)}, u32[]{:S(2)}, u32[]{:S(2)}) collective-permute-start(bf16[2,256,512]{2,1,0:T(8,128)(2,1)} %constant_dynamic-update-slice_fusion), channel_id=1, source_target_pairs={{0,2},{1,3},{2,4},{3,5},{4,6},{5,7},{6,8},{7,9},{8,10},{9,11},{10,... | collective-permute-start | bytes 1572872 | tf_op jit(solution)/shard_map/ppermute | solution.py:43
  153.6 2.6 collective-permute-start.3
  156.3 7.0 %collective-permute-done.2 = bf16[2,256,512]{2,1,0:T(8,128)(2,1)} collective-permute-done((bf16[2,256,512]{2,1,0:T(8,128)(2,1)}, bf16[2,256,512]{2,1,0:T(8,128)(2,1)}, u32[]{:S(2)}, u32[]{:S(2)}) %collective-permute-start.2) | collective-permute-done | bytes 524320 | tf_op jit(solution)/shard_map/ppermute | solution.py:43
  163.3 2.2 pad_maximum_fusion.1
  165.5 1.9 collective-permute-start.4
  167.4 7.1 %fusion.8 = (f32[256,4,8]{0,2,1:T(8,128)S(1)}, f32[4,512,256,8]{2,1,3,0:T(8,128)}) fusion(pred[256,512]{0,1:T(8,128)(4,1)S(1)} %get-tuple-element.40, bf16[256,4,8,128]{3,0,2,1:T(8,128)(2,1)S(1)} %bitcast.127, bf16[512,4,128,1]{2,1,0,3:T(4,128)(2,1)S(1)} %bitcast.133), kind=kOutput, calls=%fused_computation.16 | convolution fusion | flops 1086316544 | bytes 19562496 | tf_op jit(solution)/shard_map/thgd,shd->thgs/dot_general | solution.py:72
  174.6 2.0 reshape.606
  176.5 2.2 pad_maximum_fusion.2
  178.7 4.7 %collective-permute-start.5 = (bf16[4,256,512]{2,1,0:T(8,128)(2,1)}, bf16[4,256,512]{2,1,0:T(8,128)(2,1)}, u32[]{:S(2)}, u32[]{:S(2)}) collective-permute-start(bf16[4,256,512]{2,1,0:T(8,128)(2,1)} %pad_maximum_fusion.2), channel_id=1, source_target_pairs={{0,4},{1,5},{2,6},{3,7},{4,8},{5,9},{6,10},{7,11},{8,12},{9,13},{1... | collective-permute-start | bytes 3145736 | tf_op jit(solution)/shard_map/ppermute | solution.py:43
  184.6 2.0 reshape.607
  186.5 7.1 %fusion.9 = (f32[256,4,8]{0,2,1:T(8,128)S(1)}, f32[4,512,256,8]{2,1,3,0:T(8,128)}) fusion(pred[256,512]{0,1:T(8,128)(4,1)S(1)} %get-tuple-element.43, bf16[256,4,8,128]{3,0,2,1:T(8,128)(2,1)S(1)} %bitcast.128, bf16[512,4,128,1]{2,1,0,3:T(4,128)(2,1)S(1)} %bitcast.136), kind=kOutput, calls=%fused_computation.17 | convolution fusion | flops 1086316544 | bytes 19562496 | tf_op jit(solution)/shard_map/thgd,shd->thgs/dot_general | solution.py:72
  193.6 49.1 %collective-permute-done.4 = bf16[4,256,512]{2,1,0:T(8,128)(2,1)} collective-permute-done((bf16[4,256,512]{2,1,0:T(8,128)(2,1)}, bf16[4,256,512]{2,1,0:T(8,128)(2,1)}, u32[]{:S(2)}, u32[]{:S(2)}) %collective-permute-start.4) | collective-permute-done | bytes 1048608 | tf_op jit(solution)/shard_map/ppermute | solution.py:43
  242.7 2.1 fusion.57
  246.9 8.2 %fusion.11 = (f32[256,4,8]{0,2,1:T(8,128)S(1)}, f32[4,512,256,8]{2,1,3,0:T(8,128)}) fusion(pred[256,512]{0,1:T(8,128)(4,1)S(1)} %get-tuple-element.42, bf16[256,4,8,128]{3,0,2,1:T(8,128)(2,1)S(1)} %bitcast.129, bf16[512,4,128,1]{2,1,0,3:T(4,128)(2,1)} %bitcast.135), kind=kOutput, calls=%fused_computation.19 | convolution fusion | flops 1086316544 | bytes 19562496 | tf_op jit(solution)/shard_map/thgd,shd->thgs/dot_general | solution.py:72
  255.1 7.1 %fusion.10 = (f32[256,4,8]{0,2,1:T(8,128)S(1)}, f32[4,512,256,8]{2,1,3,0:T(8,128)}) fusion(pred[256,512]{0,1:T(8,128)(4,1)S(1)} %get-tuple-element.41, bf16[256,4,8,128]{3,0,2,1:T(8,128)(2,1)S(1)} %bitcast.130, bf16[512,4,128,1]{2,1,0,3:T(4,128)(2,1)S(1)} %bitcast.134), kind=kOutput, calls=%fused_computation.18 | convolution fusion | flops 1086316544 | bytes 19562496 | tf_op jit(solution)/shard_map/thgd,shd->thgs/dot_general | solution.py:72
  262.2 9.4 %fusion = f32[256,4,8]{0,2,1:T(8,128)S(1)} fusion(f32[4,512,256,8]{2,1,3,0:T(8,128)} %get-tuple-element.121, f32[256,4,8]{0,2,1:T(8,128)S(1)} %get-tuple-element.35, pred[256,512]{0,1:T(8,128)(4,1)S(1)} %get-tuple-element.40), kind=kLoop, calls=%fused_computation.8 | loop fusion | flops 16769024 | bytes 16973824 | tf_op jit(solution)/shard_map/reduce_sum | solution.py:82
  271.6 11.8 %fusion.18 = f32[4,128,256,8]{2,1,3,0:T(8,128)} fusion(f32[4,512,256,8]{2,1,3,0:T(8,128)} %get-tuple-element.121, f32[256,4,8]{0,2,1:T(8,128)S(1)} %get-tuple-element.35, pred[256,512]{0,1:T(8,128)(4,1)S(1)} %get-tuple-element.40, bf16[512,4,128,1]{2,1,0,3:T(4,128)(2,1)S(1)} %bitcast.141), kind=kOutput, calls=%fused_computation.23 | convolution fusion | flops 1090519040 | bytes 21659648 | tf_op jit(solution)/shard_map/thgs,shd->thgd/dot_general | solution.py:83
  283.4 11.7 %fusion.16 = f32[4,128,256,8]{2,1,3,0:T(8,128)} fusion(f32[4,512,256,8]{2,1,3,0:T(8,128)} %get-tuple-element.119, f32[256,4,8]{0,2,1:T(8,128)S(1)} %get-tuple-element.21, pred[256,512]{0,1:T(8,128)(4,1)S(1)} %get-tuple-element.43, bf16[512,4,128,1]{2,1,0,3:T(4,128)(2,1)S(1)} %bitcast.142), kind=kOutput, calls=%fused_computation.22 | convolution fusion | flops 1090519040 | bytes 21659648 | tf_op jit(solution)/shard_map/thgs,shd->thgd/dot_general | solution.py:83
  295.1 9.5 %fusion.2 = f32[256,4,8]{0,2,1:T(8,128)S(1)} fusion(f32[4,512,256,8]{2,1,3,0:T(8,128)} %get-tuple-element.119, f32[256,4,8]{0,2,1:T(8,128)S(1)} %get-tuple-element.21, pred[256,512]{0,1:T(8,128)(4,1)S(1)} %get-tuple-element.43), kind=kLoop, calls=%fused_computation.10 | loop fusion | flops 16769024 | bytes 16973824 | tf_op jit(solution)/shard_map/reduce_sum | solution.py:82
  305.9 9.3 %fusion.4 = f32[256,4,8]{0,2,1:T(8,128)S(1)} fusion(f32[4,512,256,8]{2,1,3,0:T(8,128)} %get-tuple-element.117, f32[256,4,8]{0,2,1:T(8,128)S(1)} %get-tuple-element.20, pred[256,512]{0,1:T(8,128)(4,1)S(1)} %get-tuple-element.41), kind=kLoop, calls=%fused_computation.12 | loop fusion | flops 16769024 | bytes 16973824 | tf_op jit(solution)/shard_map/reduce_sum | solution.py:82
  315.2 11.7 %fusion.14 = f32[4,128,256,8]{2,1,3,0:T(8,128)} fusion(f32[4,512,256,8]{2,1,3,0:T(8,128)} %get-tuple-element.117, f32[256,4,8]{0,2,1:T(8,128)S(1)} %get-tuple-element.20, pred[256,512]{0,1:T(8,128)(4,1)S(1)} %get-tuple-element.41, bf16[512,4,128,1]{2,1,0,3:T(4,128)(2,1)S(1)} %bitcast.144), kind=kOutput, calls=%fused_computation.21 | convolution fusion | flops 1090519040 | bytes 21659648 | tf_op jit(solution)/shard_map/thgs,shd->thgd/dot_general | solution.py:83
  327.1 9.5 %fusion.6 = f32[256,4,8]{0,2,1:T(8,128)S(1)} fusion(f32[4,512,256,8]{2,1,3,0:T(8,128)} %get-tuple-element.115, f32[256,4,8]{0,2,1:T(8,128)S(1)} %get-tuple-element.19, pred[256,512]{0,1:T(8,128)(4,1)S(1)} %get-tuple-element.42), kind=kLoop, calls=%fused_computation.14 | loop fusion | flops 16769024 | bytes 16973824 | tf_op jit(solution)/shard_map/reduce_sum | solution.py:82
  336.7 12.0 %fusion.25 = bf16[256,4,8,128]{0,3,2,1:T(8,128)(2,1)S(1)} fusion(f32[4,128,256,8]{2,1,3,0:T(8,128)} %fusion.14, f32[4,128,256,8]{2,1,3,0:T(8,128)} %fusion.16, f32[4,128,256,8]{2,1,3,0:T(8,128)} %fusion.18, f32[4,512,256,8]{2,1,3,0:T(8,128)} %get-tuple-element.115, f32[256,4,8]{0,2,1:T(8,128)S(1)} %get-tuple-element.19, ...), kind=kOutput, calls=%fused_computation.30 | convolution fusion | flops 1099956224 | bytes 32309248 | tf_op jit(solution)/shard_map/thgs,shd->thgd/dot_general | solution.py:83
  348.6 2.9 copy.31
  (83 shorter events, 49.7 us)
Async XLA Ops:
  128.4 15.0 %collective-permute-start = (bf16[1,256,512]{2,1,0:T(8,128)(2,1)S(1)}, bf16[1,256,512]{2,1,0:T(8,128)(2,1)S(1)}, u32[]{:S(2)}, u32[]{:S(2)}) collective-permute-start(bf16[1,256,512]{2,1,0:T(8,128)(2,1)S(1)} %convert_element_type.47), channel_id=1, source_target_pairs={{0,1},{1,2},{2,3},{3,4},{4,5},{5,6},{6,7},{7,8},{8,9},{9,10},{10,1... | collective-permute-start | bytes 786440 | tf_op jit(solution)/shard_map/ppermute | solution.py:43
  130.3 21.4 %collective-permute-start.1 = (bf16[1,256,512]{2,1,0:T(8,128)(2,1)}, bf16[1,256,512]{2,1,0:T(8,128)(2,1)}, u32[]{:S(2)}, u32[]{:S(2)}) collective-permute-start(bf16[1,256,512]{2,1,0:T(8,128)(2,1)} %bitcast.138), channel_id=1, source_target_pairs={{0,1},{1,2},{2,3},{3,4},{4,5},{5,6},{6,7},{7,8},{8,9},{9,10},{10,1... | collective-permute-start | bytes 786440 | tf_op jit(solution)/shard_map/ppermute | solution.py:43
  143.4 4.6 %copy-start = (bf16[1,256,512]{2,1,0:T(8,128)(2,1)}, bf16[1,256,512]{2,1,0:T(8,128)(2,1)S(1)}, u32[]{:S(2)}) copy-start(bf16[1,256,512]{2,1,0:T(8,128)(2,1)S(1)} %collective-permute-done) | copy-start | bytes 786436
  144.1 19.1 %collective-permute-start.2 = (bf16[2,256,512]{2,1,0:T(8,128)(2,1)}, bf16[2,256,512]{2,1,0:T(8,128)(2,1)}, u32[]{:S(2)}, u32[]{:S(2)}) collective-permute-start(bf16[2,256,512]{2,1,0:T(8,128)(2,1)} %constant_dynamic-update-slice_fusion), channel_id=1, source_target_pairs={{0,2},{1,3},{2,4},{3,5},{4,6},{5,7},{6,8},{7,9},{8,10},{9,11},{10,... | collective-permute-start | bytes 1572872 | tf_op jit(solution)/shard_map/ppermute | solution.py:43
  153.6 22.9 %collective-permute-start.3 = (bf16[2,256,512]{2,1,0:T(8,128)(2,1)}, bf16[2,256,512]{2,1,0:T(8,128)(2,1)}, u32[]{:S(2)}, u32[]{:S(2)}) collective-permute-start(bf16[2,256,512]{2,1,0:T(8,128)(2,1)} %pad_maximum_fusion.3), channel_id=1, source_target_pairs={{0,2},{1,3},{2,4},{3,5},{4,6},{5,7},{6,8},{7,9},{8,10},{9,11},{10,... | collective-permute-start | bytes 1572872 | tf_op jit(solution)/shard_map/ppermute | solution.py:43
  165.5 77.2 %collective-permute-start.4 = (bf16[4,256,512]{2,1,0:T(8,128)(2,1)}, bf16[4,256,512]{2,1,0:T(8,128)(2,1)}, u32[]{:S(2)}, u32[]{:S(2)}) collective-permute-start(bf16[4,256,512]{2,1,0:T(8,128)(2,1)} %pad_maximum_fusion.1), channel_id=1, source_target_pairs={{0,4},{1,5},{2,6},{3,7},{4,8},{5,9},{6,10},{7,11},{8,12},{9,13},{1... | collective-permute-start | bytes 3145736 | tf_op jit(solution)/shard_map/ppermute | solution.py:43
  167.4 9.1 %copy-start.1 = (bf16[256,512]{1,0:T(8,128)(2,1)S(1)}, bf16[256,512]{1,0:T(8,128)(2,1)}, u32[]{:S(2)}) copy-start(bf16[256,512]{1,0:T(8,128)(2,1)} %param.6) | copy-start | bytes 786436
  178.7 125.8 %collective-permute-start.5 = (bf16[4,256,512]{2,1,0:T(8,128)(2,1)}, bf16[4,256,512]{2,1,0:T(8,128)(2,1)}, u32[]{:S(2)}, u32[]{:S(2)}) collective-permute-start(bf16[4,256,512]{2,1,0:T(8,128)(2,1)} %pad_maximum_fusion.2), channel_id=1, source_target_pairs={{0,4},{1,5},{2,6},{3,7},{4,8},{5,9},{6,10},{7,11},{8,12},{9,13},{1... | collective-permute-start | bytes 3145736 | tf_op jit(solution)/shard_map/ppermute | solution.py:43
  262.2 9.4 %copy-start.2 = (bf16[512,4,128]{2,1,0:T(4,128)(2,1)S(1)}, bf16[512,4,128]{2,1,0:T(4,128)(2,1)}, u32[]{:S(2)}) copy-start(bf16[512,4,128]{2,1,0:T(4,128)(2,1)} %reshape.606) | copy-start | bytes 1572868
  271.6 11.8 %copy-start.3 = (bf16[512,4,128]{2,1,0:T(4,128)(2,1)S(1)}, bf16[512,4,128]{2,1,0:T(4,128)(2,1)}, u32[]{:S(2)}) copy-start(bf16[512,4,128]{2,1,0:T(4,128)(2,1)} %reshape.607) | copy-start | bytes 1572868
where the time goes:
time: 358 us; the launch traced here: 352 us
  matrix products  76.7 us (21%)
  other arithmetic  71.3 us (20%)
  waiting for transfers between devices  56.1 us (16%)
  between operations  54.7 us (15%)
  local copies, waits for them, and re-layouts  38.3 us (11%)
  blocking collectives  36.6 us (10%)
  starting transfers between devices  18 us (5%)
    ppermute x6, waiting for transfers between devices, shifted(): return lax.ppermute(shard, axis, pairs)  56.1 us
    dot_general x4, matrix products, attend_block(): jnp.einsum('thgs,shd->thgd', weights.astype(jnp.bfloat16), value_slice, p...  47.2 us
    reduce_sum x4, other arithmetic, attend_block(): row_total = row_total * fade + jnp.sum(weights, axis=-1)  37.6 us
    unnamed x3, blocking collectives  36.6 us
    dot_general x4, matrix products, attend_block(): jnp.einsum('thgd,shd->thgs', query_grid, key_slice, preferred_element_typ...  29.5 us
    unnamed x38, local copies, waits for them, and re-layouts  20.6 us
    ppermute x6, starting transfers between devices, shifted(): return lax.ppermute(shard, axis, pairs)  18 us
    select_n x7, other arithmetic, join_runs(): jnp.where(later[1] < 0, earlier[2], jnp.where(carried, earlier[2], later[...  12 us
  transfers between devices with their start and end apart: 6, of which 2 were waited for; matrix products, arithmetic and copies ran while one was open for 29% of the time, Pallas kernels for 0%

commit v1 on v0

v1 whole, which is shorter than its diff:
```python
import functools

import jax
import jax.numpy as jnp
import numpy as np
from jax import lax
from jax.experimental import pallas as pl
from jax.experimental.pallas import tpu as pltpu
from jax.sharding import PartitionSpec as P

HD = 128
SPAN = 7
REACH = 4
ROPE_BASE = 1000000.0
SCALE = float(HD ** (-0.5) * np.log2(np.e))
BIG = float(2.0**100)


def rotate(x, cosine, signed_sine):
    x = x.astype(jnp.float32)
    return x * cosine + pltpu.roll(x, HD // 2, 1) * signed_sine


def kernel(
    kv_heads,
    group,
    seg_in,
    q_in,
    k_in,
    v_in,
    table_in,
    freq_in,
    out,
    rk_out,
    segs,
    qraw,
    kv,
    tables,
    freq,
    qt,
    qaug,
    diag,
    own_cos,
    own_sin,
    blk_cos,
    blk_sin,
    kx,
    kaug,
    vt,
    top,
    total,
    acc,
    ovm,
    rkvm,
    in_sem,
    seg_send,
    seg_recv,
    hop_send,
    side_send,
    kv_recv,
    out_sem,
):
    rows = q_in.shape[0]
    half = HD // 2
    me = lax.axis_index("seq")
    n = lax.axis_size("seq")
    core = lax.rem(me, 2)
    own_slot = 1 - core

    def device(offset):
        return {"seq": lax.rem(me + offset + n, n)}

    seg_load = pltpu.make_async_copy(seg_in, segs.at[0], in_sem.at[0])
    seg_load.start()
    kv_loads = []
    for h in range(kv_heads):
        cols = slice(h * HD, (h + 1) * HD)
        for w, src in ((0, k_in), (1, v_in)):
            load = pltpu.make_async_copy(
                src.at[:, cols], kv.at[own_slot, h, w], in_sem.at[4 + 2 * h + w]
            )
            load.start()
            kv_loads.append(load)
    freq_load = pltpu.make_async_copy(freq_in, freq, in_sem.at[1])
    freq_load.start()
    table_load = pltpu.make_async_copy(table_in, tables, in_sem.at[2])
    table_load.start()
    q_load = pltpu.make_async_copy(q_in, qraw, in_sem.at[3])
    q_load.start()

    barrier = pltpu.get_barrier_semaphore()
    for o in range(1, SPAN + 1):
        pl.semaphore_signal(barrier, 1, device_id=device(o))
        pl.semaphore_signal(barrier, 1, device_id=device(-o))
    pl.semaphore_wait(barrier, 2 * SPAN)

    seg_load.wait()
    seg_copies = []
    for o in range(1, SPAN + 1):
        copy = pltpu.make_async_remote_copy(
            src_ref=segs.at[0],
            dst_ref=segs.at[o],
            send_sem=seg_send.at[o - 1],
            recv_sem=seg_recv.at[o - 1],
            device_id=device(o),
        )
        copy.start()
        seg_copies.append(copy)

    def hop(slot, j, h):
        return pltpu.make_async_remote_copy(
            src_ref=kv.at[slot, h],
            dst_ref=kv.at[slot + 2, h],
            send_sem=hop_send.at[j, h],
            recv_sem=kv_recv.at[slot + 2, h],
            device_id=device(2),
        )

    def last_hop(slot, h):
        return pltpu.make_async_remote_copy(
            src_ref=kv.at[slot, h],
            dst_ref=kv.at[slot + 2, h],
            send_sem=hop_send.at[REACH - 1, h],
            recv_sem=kv_recv.at[slot + 2, h],
            device_id=device(1),
        )

    def side(slot, j, h):
        return pltpu.make_async_remote_copy(
            src_ref=kv.at[slot, h],
            dst_ref=kv.at[slot, h],
            send_sem=side_send.at[j, h],
            recv_sem=kv_recv.at[slot, h],
            device_id=device(1 - 2 * core),
        )

    for h in range(kv_heads):
        kv_loads[2 * h].wait()
        kv_loads[2 * h + 1].wait()
        hop(own_slot, 0, h).start()

        @pl.when(core == 0)
        def _():
            side(own_slot, 0, h).start()

    freq_load.wait()
    table_load.wait()
    lane = lax.broadcasted_iota(jnp.int32, (rows, HD), 1)
    sublane = lax.broadcasted_iota(jnp.int32, (rows, HD), 0).astype(jnp.float32)
    sign = jnp.where(lane < half, -1.0, 1.0)
    freq_row = freq[...]
    seg_row = segs[0]
    seg_first = seg_row[:, :1]
    first_row = seg_row == seg_first
    seg_wide = jnp.broadcast_to(seg_row.astype(jnp.float32), (rows, rows))
    seg_tall = seg_wide.T
    key_at = lax.broadcasted_iota(jnp.int32, (rows, rows), 0)
    row_at = lax.broadcasted_iota(jnp.int32, (rows, rows), 1)
    same = seg_tall == seg_wide
    diag[...] = jnp.where(same & (key_at <= row_at), 0.0, -BIG)
    local_position = jnp.sum(
        jnp.where(same & (row_at < key_at), 1.0, 0.0), axis=1, keepdims=True
    )
    first_tall = seg_tall[:, :HD] == seg_first.astype(jnp.float32)
    local_angle = local_position * freq_row
    local_cos = jnp.cos(local_angle)
    local_sin = jnp.sin(local_angle)
    aug_at = lax.broadcasted_iota(jnp.int32, (HD, rows), 0)
    qaug[...] = jnp.where(aug_at == 0, -BIG, 0.0).astype(jnp.bfloat16)

    for copy in seg_copies:
        copy.wait_recv()
    hits = jnp.zeros_like(seg_row, jnp.float32)
    for o in range(1, SPAN + 1):
        hits += jnp.where(segs[o] == seg_first, 1.0, 0.0)
    before = jnp.sum(hits, axis=1, keepdims=True)
    base_angle = before * freq_row
    base_cos = jnp.where(first_tall, jnp.cos(base_angle), 1.0)
    base_sin = jnp.where(first_tall, jnp.sin(base_angle), 0.0)
    own_cos[...] = local_cos * base_cos - local_sin * base_sin
    own_sin[...] = (local_sin * base_cos + local_cos * base_sin) * sign

    for h in range(kv_heads):
        rkvm[:, h * HD : (h + 1) * HD] = rotate(
            kv[own_slot, h, 0], own_cos[...], own_sin[...]
        ).astype(jnp.bfloat16)
    rk_store = pltpu.make_async_copy(rkvm, rk_out, in_sem.at[0])
    rk_store.start()

    q_load.wait()

    def turn(t, carry):
        at = pl.multiple_of(t * HD, HD)
        turned = rotate(qraw[:, pl.ds(at, HD)], own_cos[...], own_sin[...])
        qt[t] = turned.astype(jnp.bfloat16).T
        return carry

    lax.fori_loop(0, kv_heads * group, turn, 0)

    def own_head(h):
        vt[:, :rows] = kv[own_slot, h, 1].T

        def tile(g, carry):
            t = h * group + g
            scores = jnp.dot(
                rkvm[:, h * HD : (h + 1) * HD], qt[t], preferred_element_type=jnp.float32
            )
            scores = scores + diag[...]
            peak = jnp.max(scores, axis=0, keepdims=True)
            weights = jnp.exp2(scores * SCALE - peak * SCALE)
            top[t] = peak
            total[t] = jnp.sum(weights.reshape(rows // 8, 8, rows), axis=0)
            acc[t] = jnp.dot(
                vt[:, :rows], weights.astype(jnp.bfloat16), preferred_element_type=jnp.float32
            )
            return carry

        lax.fori_loop(0, group, tile, 0, unroll=2)

    for h in range(kv_heads):
        own_head(h)

    def prepare(slot, part):
        offset = ((slot - 1 + core) * rows).astype(jnp.float32)
        angle = (before - offset) * freq_row
        c, s = jnp.cos(angle), jnp.sin(angle)
        blk_cos[part] = tables[0] * c - tables[1] * s
        blk_sin[part] = (tables[1] * c + tables[0] * s) * sign
        invalid = (sublane < offset - before) & (lane == 0)
        kaug[part * rows : (part + 1) * rows] = jnp.where(invalid, 1.0, 0.0).astype(jnp.bfloat16)

    def unpack(slot, h, part):
        span = slice(part * rows, (part + 1) * rows)
        kx[span] = rotate(kv[slot, h, 0], blk_cos[part], blk_sin[part]).astype(jnp.bfloat16)
        vt[:, span] = kv[slot, h, 1].T

    def attend(h, depth):
        def tile(g, carry):
            t = h * group + g
            scores = jnp.dot(
                jnp.concatenate([kx[:depth], kaug[:depth]], axis=1),
                jnp.concatenate([qt[t], qaug[...]], axis=0),
                preferred_element_type=jnp.float32,
            )
            old = top[t]
            peak = jnp.where(
                first_row, jnp.maximum(old, jnp.max(scores, axis=0, keepdims=True)), old
            )
            fade = jnp.exp2((old - peak) * SCALE)
            shift = jnp.where(first_row, peak * SCALE, BIG)
            weights = jnp.exp2(scores * SCALE - shift)
            top[t] = peak
            total[t] = total[t] * fade + jnp.sum(
                weights.reshape(depth // 8, 8, rows), axis=0
            )
            acc[t] = acc[t] * fade + jnp.dot(
                vt[:, :depth], weights.astype(jnp.bfloat16), preferred_element_type=jnp.float32
            )
            return carry

        lax.fori_loop(0, group, tile, 0, unroll=2)

    def store(h):
        return pltpu.make_async_copy(
            ovm.at[h], out.at[:, h * group * HD : (h + 1) * group * HD], out_sem.at[h]
        )

    def finish(h):
        for g in range(group):
            t = h * group + g
            share = 1.0 / jnp.sum(total[t], axis=0, keepdims=True)
            ovm[h, :, g * HD : (g + 1) * HD] = (acc[t] * share).astype(jnp.bfloat16).T
        store(h).start()

    @pl.when(core == 1)
    def _():
        prepare(1, 0)
        for h in range(kv_heads):
            side(1, 0, h).wait_recv()
            unpack(1, h, 0)
            attend(h, rows)

    for j in range(1, REACH):
        direct = 2 * j + 1 - core
        other = 2 * j + core
        prepare(direct, 0)
        prepare(other, 1)
        for h in range(kv_heads):
            hop(direct - 2, j - 1, h).wait_recv()
            side(direct, j, h).start()
            if j < REACH - 1:
                hop(direct, j, h).start()
            else:

                @pl.when(core == 1)
                def _():
                    last_hop(direct, h).start()

            unpack(direct, h, 0)
            side(other, j, h).wait_recv()
            unpack(other, h, 1)
            attend(h, 2 * rows)
            if j == REACH - 1:

                @pl.when(core == 1)
                def _():
                    finish(h)

    @pl.when(core == 0)
    def _():
        last = 2 * REACH
        prepare(last, 0)
        for h in range(kv_heads):
            last_hop(last - 2, h).wait_recv()
            unpack(last, h, 0)
            attend(h, rows)
            finish(h)

    for copy in seg_copies:
        copy.wait_send()
    for h in range(kv_heads):
        for j in range(REACH - 1):
            hop(0, j, h).wait_send()
        for j in range(1, REACH):
            side(0, j, h).wait_send()

        @pl.when(core == 0)
        def _():
            side(0, 0, h).wait_send()

        @pl.when(core == 1)
        def _():
            last_hop(0, h).wait_send()

        store(h).wait()
    rk_store.wait()


def local(queries, keys, values, segment_ids):
    rows, width = queries.shape
    kv_width = keys.shape[1]
    heads, kv_heads = width // HD, kv_width // HD
    group = heads // kv_heads
    half = HD // 2
    freq = (ROPE_BASE ** (-(np.arange(half) * (2.0 / HD)))).astype(np.float32)
    freq = np.concatenate([freq, freq])[None]
    angle = (np.arange(rows, dtype=np.float32)[:, None] * freq).astype(np.float64)
    table = np.stack([np.cos(angle), np.sin(angle)]).astype(np.float32)
    any_space = pl.BlockSpec(memory_space=pl.ANY)
    bf16, f32 = jnp.bfloat16, jnp.float32
    slots = 2 * REACH + 1
    dma = pltpu.SemaphoreType.DMA
    return pl.pallas_call(
        functools.partial(kernel, kv_heads, group),
        out_shape=(
            jax.ShapeDtypeStruct((rows, width), bf16),
            jax.ShapeDtypeStruct((rows, kv_width), bf16),
        ),
        in_specs=[any_space] * 6,
        out_specs=(any_space, any_space),
        scratch_shapes=[
            pltpu.VMEM((SPAN + 1, 1, rows), jnp.int32),
            pltpu.VMEM((rows, width), bf16),
            pltpu.VMEM((slots, kv_heads, 2, rows, HD), bf16),
            pltpu.VMEM((2, rows, HD), f32),
            pltpu.VMEM((1, HD), f32),
            pltpu.VMEM((heads, HD, rows), bf16),
            pltpu.VMEM((HD, rows), bf16),
            pltpu.VMEM((rows, rows), f32),
            pltpu.VMEM((rows, HD), f32),
            pltpu.VMEM((rows, HD), f32),
            pltpu.VMEM((2, rows, HD), f32),
            pltpu.VMEM((2, rows, HD), f32),
            pltpu.VMEM((2 * rows, HD), bf16),
            pltpu.VMEM((2 * rows, HD), bf16),
            pltpu.VMEM((HD, 2 * rows), bf16),
            pltpu.VMEM((heads, 1, rows), f32),
            pltpu.VMEM((heads, 8, rows), f32),
            pltpu.VMEM((heads, HD, rows), f32),
            pltpu.VMEM((kv_heads, rows, group * HD), bf16),
            pltpu.VMEM((rows, kv_width), bf16),
            dma((4 + 2 * kv_heads,)),
            dma((SPAN,)),
            dma((SPAN,)),
            dma((REACH, kv_heads)),
            dma((REACH, kv_heads)),
            dma((slots, kv_heads)),
            dma((kv_heads,)),
        ],
        compiler_params=pltpu.CompilerParams(
            collective_id=0, has_side_effects=True, vmem_limit_bytes=56 * 1024 * 1024
        ),
    )(
        segment_ids.reshape(1, rows),
        queries,
        keys,
        values,
        jnp.asarray(table),
        jnp.asarray(freq),
    )


def solution(mesh):
    both = ("groups", "seq")
    return jax.shard_map(
        local,
        mesh=mesh,
        in_specs=(P(both, None), P(both, None), P(both, None), P(both)),
        out_specs=(P(both, None), P(both, None)),
        check_vma=False,
    )
```

time: 358 us -> 137 us (0.38)
  the two profiles are of different devices: /device:TPU:528 before, /device:TPU:514 now
where the time goes in v1:
time: 137 us
  Pallas kernels  132 us (96%)
  local copies, waits for them, and re-layouts  3.88 us (3%)
    pallas_call x1, Pallas kernels, local(): pl.pallas_call(functools.partial(kernel, kv_heads, group), out_shape=(jax...  132 us
    unnamed x4, local copies, waits for them, and re-layouts  3.88 us

profile of v1, /device:TPU:514, one launch (start us, length us, event | category | flops | bytes accessed | tf_op | source)
XLA Modules:
  0.0 136.8 jit_solution(8291195833635149107)
XLA Ops:
  0.6 132.3 %shard_map.77 = (bf16[256,4096]{1,0:T(8,128)(2,1)}, bf16[256,512]{1,0:T(8,128)(2,1)}) custom-call(s32[1,256]{1,0:T(1,128)} %bitcast.1, bf16[256,4096]{1,0:T(8,128)(2,1)} %q_in.1, bf16[256,512]{1,0:T(8,128)(2,1)} %k_in.1, bf16[256,512]{1,0:T(8,128)(2,1)} %v_in.1, f32[2,256,128]{2,1,0:T(8,128)} %constant.4.clone.table_in, f32[1,128]{1,0:T(1,128)} %constant.5.clone.freq_in), custom_call_target="tpu_custom_call" | custom-call | tf_op jit(solution)/shard_map/pallas_call | solution.py:353
  132.9 0.0 copy-start
  132.9 3.2 %copy.10 = bf16[256,4096]{1,0:T(8,128)(2,1)} copy(bf16[256,4096]{1,0:T(8,128)(2,1)} %get-tuple-element.4) | data formatting | bytes 4194304
  136.1 0.0 copy-done
  136.1 0.7 copy.11
Async XLA Ops:
  132.9 3.2 %copy-start = (bf16[256,512]{1,0:T(8,128)(2,1)S(1)}, bf16[256,512]{1,0:T(8,128)(2,1)}, u32[]{:S(2)}) copy-start(bf16[256,512]{1,0:T(8,128)(2,1)} %get-tuple-element.5) | copy-start | bytes 786436

commit v2 on v1

--- a/solution.py
+++ b/solution.py
@@ -11,6 +11,7 @@
 HD = 128
 SPAN = 7
 REACH = 4
+WIDE = 2
 ROPE_BASE = 1000000.0
 SCALE = float(HD ** (-0.5) * np.log2(np.e))
 BIG = float(2.0**100)
@@ -50,6 +51,10 @@
     top,
     total,
     acc,
+    raw,
+    peaks,
+    rounded,
+    fades,
     ovm,
     rkvm,
     in_sem,
@@ -166,7 +171,18 @@
     local_cos = jnp.cos(local_angle)
     local_sin = jnp.sin(local_angle)
     aug_at = lax.broadcasted_iota(jnp.int32, (HD, rows), 0)
-    qaug[...] = jnp.where(aug_at == 0, -BIG, 0.0).astype(jnp.bfloat16)
+    later_row = jnp.where(first_row, 0.0, -BIG)
+    qaug[...] = jnp.where(
+        aug_at == 0, -BIG, jnp.where(aug_at == 1, later_row, 0.0)
+    ).astype(jnp.bfloat16)
+
+    def clear(t, carry):
+        top[t] = jnp.full((1, rows), -4.0 * BIG, jnp.float32)
+        total[t] = jnp.zeros((8, rows), jnp.float32)
+        acc[t] = jnp.zeros((HD, rows), jnp.float32)
+        return carry
+
+    lax.fori_loop(0, kv_heads * group, clear, 0)
 
     for copy in seg_copies:
         copy.wait_recv()
@@ -197,72 +213,112 @@
 
     lax.fori_loop(0, kv_heads * group, turn, 0)
 
-    def own_head(h):
-        vt[:, :rows] = kv[own_slot, h, 1].T
-
-        def tile(g, carry):
-            t = h * group + g
+    wide_rows = 2 * rows
+    per_chunk = group // WIDE
+    per_pair = kv_heads * per_chunk
+    steps = (SPAN + 1) // 2 * per_pair
+
+    def prepare(pair):
+        for part in range(2):
+            offset = 2 * pair + part
+            distance = (offset * rows).astype(jnp.float32)
+            angle = (before - distance) * freq_row
+            c, s = jnp.cos(angle), jnp.sin(angle)
+            own = offset == 0
+
+            @pl.when(own)
+            def _():
+                blk_cos[part] = own_cos[...]
+                blk_sin[part] = own_sin[...]
+
+            @pl.when(jnp.logical_not(own))
+            def _():
+                blk_cos[part] = tables[0] * c - tables[1] * s
+                blk_sin[part] = (tables[1] * c + tables[0] * s) * sign
+
+            earlier = jnp.where(own, 0.0, 1.0)
+            invalid = (sublane < distance - before) & (lane == 0)
+            kaug[part * rows : (part + 1) * rows] = jnp.where(
+                invalid, 1.0, jnp.where(lane == 1, earlier, 0.0)
+            ).astype(jnp.bfloat16)
+
+    def unpack(slot, h, part, buf):
+        span = slice(part * rows, (part + 1) * rows)
+        kx[buf, span] = rotate(kv[slot, h, 0], blk_cos[part], blk_sin[part]).astype(jnp.bfloat16)
+        vt[buf, :, span] = kv[slot, h, 1].T
+
+    def chunk(q):
+        pair, h = q // kv_heads, lax.rem(q, kv_heads)
+        buf = lax.rem(q, 2)
+        ahead = 2 * pair + 3 - core
+
+        @pl.when(pair < REACH - 1)
+        def _():
+            hop(ahead - 2, pair, h).wait_recv()
+            side(ahead, pair + 1, h).start()
+
+        @pl.when(pair < REACH - 2)
+        def _():
+            hop(ahead, pair + 1, h).start()
+
+        @pl.when((pair == REACH - 2) & (core == 1))
+        def _():
+            last_hop(ahead, h).start()
+
+        @pl.when(h == 0)
+        def _():
+            prepare(pair)
+
+        unpack(2 * pair + 1 - core, h, 0, buf)
+        other = 2 * pair + 2 - core
+        side(other, 0, h).wait_recv()
+        unpack(other, h, 1, buf)
+
+    def score(s, own):
+        buf = lax.rem(s // per_chunk, 2)
+        for u in range(WIDE):
+            t = lax.rem(s, per_pair) * WIDE + u
             scores = jnp.dot(
-                rkvm[:, h * HD : (h + 1) * HD], qt[t], preferred_element_type=jnp.float32
-            )
-            scores = scores + diag[...]
-            peak = jnp.max(scores, axis=0, keepdims=True)
-            weights = jnp.exp2(scores * SCALE - peak * SCALE)
-            top[t] = peak
-            total[t] = jnp.sum(weights.reshape(rows // 8, 8, rows), axis=0)
-            acc[t] = jnp.dot(
-                vt[:, :rows], weights.astype(jnp.bfloat16), preferred_element_type=jnp.float32
-            )
-            return carry
-
-        lax.fori_loop(0, group, tile, 0, unroll=2)
-
-    for h in range(kv_heads):
-        own_head(h)
-
-    def prepare(slot, part):
-        offset = ((slot - 1 + core) * rows).astype(jnp.float32)
-        angle = (before - offset) * freq_row
-        c, s = jnp.cos(angle), jnp.sin(angle)
-        blk_cos[part] = tables[0] * c - tables[1] * s
-        blk_sin[part] = (tables[1] * c + tables[0] * s) * sign
-        invalid = (sublane < offset - before) & (lane == 0)
-        kaug[part * rows : (part + 1) * rows] = jnp.where(invalid, 1.0, 0.0).astype(jnp.bfloat16)
-
-    def unpack(slot, h, part):
-        span = slice(part * rows, (part + 1) * rows)
-        kx[span] = rotate(kv[slot, h, 0], blk_cos[part], blk_sin[part]).astype(jnp.bfloat16)
-        vt[:, span] = kv[slot, h, 1].T
-
-    def attend(h, depth):
-        def tile(g, carry):
-            t = h * group + g
-            scores = jnp.dot(
-                jnp.concatenate([kx[:depth], kaug[:depth]], axis=1),
+                jnp.concatenate([kx[buf], kaug[...]], axis=1),
                 jnp.concatenate([qt[t], qaug[...]], axis=0),
                 preferred_element_type=jnp.float32,
             )
+            low, high = scores[:rows], scores[rows:]
+            if own:
+                low = low + diag[...]
+            raw[u, :rows] = low
+            raw[u, rows:] = high
+            peaks[u] = jnp.maximum(
+                jnp.max(low.reshape(rows // 8, 8, rows), axis=0),
+                jnp.max(high.reshape(rows // 8, 8, rows), axis=0),
+            )
+
+    def weigh(s):
+        for u in range(WIDE):
+            t = lax.rem(s, per_pair) * WIDE + u
             old = top[t]
-            peak = jnp.where(
-                first_row, jnp.maximum(old, jnp.max(scores, axis=0, keepdims=True)), old
-            )
+            peak = jnp.maximum(old, jnp.max(peaks[u], axis=0, keepdims=True))
             fade = jnp.exp2((old - peak) * SCALE)
-            shift = jnp.where(first_row, peak * SCALE, BIG)
-            weights = jnp.exp2(scores * SCALE - shift)
+            weights = jnp.exp2(raw[u] * SCALE - peak * SCALE)
             top[t] = peak
             total[t] = total[t] * fade + jnp.sum(
-                weights.reshape(depth // 8, 8, rows), axis=0
+                weights.reshape(wide_rows // 8, 8, rows), axis=0
             )
-            acc[t] = acc[t] * fade + jnp.dot(
-                vt[:, :depth], weights.astype(jnp.bfloat16), preferred_element_type=jnp.float32
+            rounded[u] = weights.astype(jnp.bfloat16)
+            fades[u] = fade
+
+    def mix(s):
+        buf = lax.rem(s // per_chunk, 2)
+        for u in range(WIDE):
+            t = lax.rem(s, per_pair) * WIDE + u
+            acc[t] = acc[t] * fades[u] + jnp.dot(
+                vt[buf], rounded[u], preferred_element_type=jnp.float32
             )
-            return carry
-
-        lax.fori_loop(0, group, tile, 0, unroll=2)
 
     def store(h):
+        at = pl.multiple_of(h * group * HD, group * HD)
         return pltpu.make_async_copy(
-            ovm.at[h], out.at[:, h * group * HD : (h + 1) * group * HD], out_sem.at[h]
+            ovm.at[h], out.at[:, pl.ds(at, group * HD)], out_sem.at[h]
         )
 
     def finish(h):
@@ -272,49 +328,44 @@
             ovm[h, :, g * HD : (g + 1) * HD] = (acc[t] * share).astype(jnp.bfloat16).T
         store(h).start()
 
-    @pl.when(core == 1)
-    def _():
-        prepare(1, 0)
-        for h in range(kv_heads):
-            side(1, 0, h).wait_recv()
-            unpack(1, h, 0)
-            attend(h, rows)
-
-    for j in range(1, REACH):
-        direct = 2 * j + 1 - core
-        other = 2 * j + core
-        prepare(direct, 0)
-        prepare(other, 1)
-        for h in range(kv_heads):
-            hop(direct - 2, j - 1, h).wait_recv()
-            side(direct, j, h).start()
-            if j < REACH - 1:
-                hop(direct, j, h).start()
-            else:
-
-                @pl.when(core == 1)
-                def _():
-                    last_hop(direct, h).start()
-
-            unpack(direct, h, 0)
-            side(other, j, h).wait_recv()
-            unpack(other, h, 1)
-            attend(h, 2 * rows)
-            if j == REACH - 1:
-
-                @pl.when(core == 1)
-                def _():
-                    finish(h)
-
-    @pl.when(core == 0)
-    def _():
-        last = 2 * REACH
-        prepare(last, 0)
-        for h in range(kv_heads):
-            last_hop(last - 2, h).wait_recv()
-            unpack(last, h, 0)
-            attend(h, rows)
-            finish(h)
+    def step(s, own):
+        @pl.when(lax.rem(s, per_chunk) == 0)
+        def _():
+            chunk(s // per_chunk)
+
+        mix(s - 2)
+        weigh(s - 1)
+        score(s, own)
+
+    chunk(jnp.int32(0))
+    score(jnp.int32(0), True)
+    if per_chunk == 1:
+        chunk(jnp.int32(1))
+    weigh(jnp.int32(0))
+    score(jnp.int32(1), True)
+
+    def own_step(s, carry):
+        step(s, True)
+        return carry
+
+    lax.fori_loop(2, per_pair, own_step, 0)
+
+    def later_step(s, carry):
+        ready = s - 2 - (steps - per_pair)
+
+        @pl.when((ready > 0) & (lax.rem(ready, per_chunk) == 0))
+        def _():
+            finish(ready // per_chunk - 1)
+
+        step(s, False)
+        return carry
+
+    lax.fori_loop(per_pair, steps, later_step, 0)
+    mix(jnp.int32(steps - 2))
+    weigh(jnp.int32(steps - 1))
+    for h in range(kv_heads - 1, kv_heads):
+        mix(jnp.int32(steps - 1))
+        finish(h)
 
     for copy in seg_copies:
         copy.wait_send()
@@ -371,12 +422,16 @@
             pltpu.VMEM((rows, HD), f32),
             pltpu.VMEM((2, rows, HD), f32),
             pltpu.VMEM((2, rows, HD), f32),
+            pltpu.VMEM((2, 2 * rows, HD), bf16),
             pltpu.VMEM((2 * rows, HD), bf16),
-            pltpu.VMEM((2 * rows, HD), bf16),
-            pltpu.VMEM((HD, 2 * rows), bf16),
+            pltpu.VMEM((2, HD, 2 * rows), bf16),
             pltpu.VMEM((heads, 1, rows), f32),
             pltpu.VMEM((heads, 8, rows), f32),
             pltpu.VMEM((heads, HD, rows), f32),
+            pltpu.VMEM((WIDE, 2 * rows, rows), f32),
+            pltpu.VMEM((WIDE, 8, rows), f32),
+            pltpu.VMEM((WIDE, 2 * rows, rows), bf16),
+            pltpu.VMEM((WIDE, 1, rows), f32),
             pltpu.VMEM((kv_heads, rows, group * HD), bf16),
             pltpu.VMEM((rows, kv_width), bf16),
             dma((4 + 2 * kv_heads,)),

time: 137 us -> 76.8 us (0.56)
  the two profiles are of different devices: /device:TPU:514 before, /device:TPU:513 now
where the time goes in v2:
time: 76.8 us; the launch traced here: 76.7 us
  Pallas kernels  72.2 us (94%)
  local copies, waits for them, and re-layouts  3.88 us (5%)
    pallas_call x1, Pallas kernels, local(): pl.pallas_call(functools.partial(kernel, kv_heads, group), out_shape=(jax...  72.2 us
    unnamed x4, local copies, waits for them, and re-layouts  3.88 us

profile of v2, /device:TPU:513, one launch (start us, length us, event | category | flops | bytes accessed | tf_op | source)
XLA Modules:
  0.0 76.7 jit_solution(10130516995673527715)
XLA Ops:
  0.6 72.2 %shard_map.77 = (bf16[256,4096]{1,0:T(8,128)(2,1)}, bf16[256,512]{1,0:T(8,128)(2,1)}) custom-call(s32[1,256]{1,0:T(1,128)} %bitcast.1, bf16[256,4096]{1,0:T(8,128)(2,1)} %q_in.1, bf16[256,512]{1,0:T(8,128)(2,1)} %k_in.1, bf16[256,512]{1,0:T(8,128)(2,1)} %v_in.1, f32[2,256,128]{2,1,0:T(8,128)} %constant.4.clone.table_in, f32[1,128]{1,0:T(1,128)} %constant.5.clone.freq_in), custom_call_target="tpu_custom_call" | custom-call | tf_op jit(solution)/shard_map/pallas_call | solution.py:404
  72.8 0.0 copy-start
  72.8 3.2 %copy.10 = bf16[256,4096]{1,0:T(8,128)(2,1)} copy(bf16[256,4096]{1,0:T(8,128)(2,1)} %get-tuple-element.4) | data formatting | bytes 4194304
  76.0 0.0 copy-done
  76.0 0.7 copy.11
Async XLA Ops:
  72.8 3.2 %copy-start = (bf16[256,512]{1,0:T(8,128)(2,1)S(1)}, bf16[256,512]{1,0:T(8,128)(2,1)}, u32[]{:S(2)}) copy-start(bf16[256,512]{1,0:T(8,128)(2,1)} %get-tuple-element.5) | copy-start | bytes 786436

commit v3 on v2

--- a/solution.py
+++ b/solution.py
@@ -1,4 +1,5 @@
 import functools
+import math
 
 import jax
 import jax.numpy as jnp
@@ -12,6 +13,7 @@
 SPAN = 7
 REACH = 4
 WIDE = 2
+TURNED = 2
 ROPE_BASE = 1000000.0
 SCALE = float(HD ** (-0.5) * np.log2(np.e))
 BIG = float(2.0**100)
@@ -62,6 +64,11 @@
     seg_recv,
     hop_send,
     side_send,
+    chain_send,
+    via,
+    via_send,
+    via_recv,
+    leg_send,
     kv_recv,
     out_sem,
 ):
@@ -71,9 +78,20 @@
     n = lax.axis_size("seq")
     core = lax.rem(me, 2)
     own_slot = 1 - core
+    chip = me // 2
+    last = n // 2 - 1
+    width = math.isqrt(n // 2)
 
     def device(offset):
-        return {"seq": lax.rem(me + offset + n, n)}
+        return {"seq": me + offset}
+
+    def relay_of(source):
+        return source // width * width + lax.rem(source + width - 2, width)
+
+    def far_of(source):
+        return jnp.minimum(source + REACH, last)
+
+    relayed = chip // width * width + lax.rem(chip + 2, width)
 
     seg_load = pltpu.make_async_copy(seg_in, segs.at[0], in_sem.at[0])
     seg_load.start()
@@ -94,29 +112,50 @@
     q_load.start()
 
     barrier = pltpu.get_barrier_semaphore()
+
+    def tell(rank, when):
+        @pl.when(when)
+        def _():
+            pl.semaphore_signal(barrier, 1, device_id={"seq": rank})
+
     for o in range(1, SPAN + 1):
-        pl.semaphore_signal(barrier, 1, device_id=device(o))
-        pl.semaphore_signal(barrier, 1, device_id=device(-o))
-    pl.semaphore_wait(barrier, 2 * SPAN)
+        tell(me - o, me >= o)
+    tell(me + 1, (core == 0) & (chip >= 1))
+    tell(me + 2, (core == 0) & (chip >= 1) & (chip < last))
+    tell(2 * relayed + 1, (core == 1) & (relayed < last))
+    tell(2 * relay_of(chip - REACH) + 1, (core == 0) & (chip >= REACH))
+    for back in range(1, REACH):
+        tell(2 * relay_of(chip - back) + 1, (core == 0) & (chip == last))
+    receivers = jnp.minimum(SPAN, n - 1 - me) + jnp.where(
+        core == 0,
+        jnp.where(chip >= 2, 1, 0),
+        jnp.where(chip >= 1, 1, 0)
+        + jnp.where(chip < last, 1, 0)
+        + jnp.where(relayed < last, 1, 0),
+    )
+    pl.semaphore_wait(barrier, receivers)
 
     seg_load.wait()
-    seg_copies = []
-    for o in range(1, SPAN + 1):
-        copy = pltpu.make_async_remote_copy(
+    def seg_copy(o):
+        return pltpu.make_async_remote_copy(
             src_ref=segs.at[0],
             dst_ref=segs.at[o],
             send_sem=seg_send.at[o - 1],
             recv_sem=seg_recv.at[o - 1],
             device_id=device(o),
         )
-        copy.start()
-        seg_copies.append(copy)
-
-    def hop(slot, j, h):
+
+    for o in range(1, SPAN + 1):
+
+        @pl.when(me + o < n)
+        def _():
+            seg_copy(o).start()
+
+    def hop(slot, h):
         return pltpu.make_async_remote_copy(
             src_ref=kv.at[slot, h],
             dst_ref=kv.at[slot + 2, h],
-            send_sem=hop_send.at[j, h],
+            send_sem=hop_send.at[slot, h],
             recv_sem=kv_recv.at[slot + 2, h],
             device_id=device(2),
         )
@@ -125,28 +164,75 @@
         return pltpu.make_async_remote_copy(
             src_ref=kv.at[slot, h],
             dst_ref=kv.at[slot + 2, h],
-            send_sem=hop_send.at[REACH - 1, h],
+            send_sem=hop_send.at[slot, h],
             recv_sem=kv_recv.at[slot + 2, h],
             device_id=device(1),
         )
 
-    def side(slot, j, h):
+    def side(slot, h):
         return pltpu.make_async_remote_copy(
             src_ref=kv.at[slot, h],
             dst_ref=kv.at[slot, h],
-            send_sem=side_send.at[j, h],
+            send_sem=side_send.at[slot, h],
             recv_sem=kv_recv.at[slot, h],
             device_id=device(1 - 2 * core),
+        )
+
+    def back_hop(slot, h):
+        return pltpu.make_async_remote_copy(
+            src_ref=kv.at[slot, h],
+            dst_ref=kv.at[slot - 2, h],
+            send_sem=chain_send.at[slot, h],
+            recv_sem=kv_recv.at[slot - 2, h],
+            device_id=device(-2),
+        )
+
+    def first_leg(h):
+        return pltpu.make_async_remote_copy(
+            src_ref=kv.at[own_slot, h],
+            dst_ref=via.at[h - TURNED],
+            send_sem=via_send.at[h - TURNED],
+            recv_sem=via_recv.at[h - TURNED],
+            device_id={"seq": 2 * relay_of(chip) + 1},
+        )
+
+    def second_leg(h):
+        far = far_of(relayed)
+        slot = 2 * (far - relayed)
+        return pltpu.make_async_remote_copy(
+            src_ref=via.at[h - TURNED],
+            dst_ref=kv.at[slot, h],
+            send_sem=leg_send.at[h - TURNED],
+            recv_sem=kv_recv.at[slot, h],
+            device_id={"seq": 2 * far},
         )
 
     for h in range(kv_heads):
         kv_loads[2 * h].wait()
         kv_loads[2 * h + 1].wait()
-        hop(own_slot, 0, h).start()
+
+        @pl.when((chip < last) & ((core == 0) | (h < TURNED)))
+        def _():
+            hop(own_slot, h).start()
+
+        if h >= TURNED:
+
+            @pl.when((chip < last) & (core == 1))
+            def _():
+                first_leg(h).start()
 
         @pl.when(core == 0)
         def _():
-            side(own_slot, 0, h).start()
+            side(own_slot, h).start()
+
+    def blank(slot, carry):
+        @pl.when(chip < slot // 2)
+        def _():
+            kv[slot] = jnp.zeros(kv.shape[1:], kv.dtype)
+
+        return carry
+
+    lax.fori_loop(2, 2 * REACH + 1, blank, 0)
 
     freq_load.wait()
     table_load.wait()
@@ -184,8 +270,16 @@
 
     lax.fori_loop(0, kv_heads * group, clear, 0)
 
-    for copy in seg_copies:
-        copy.wait_recv()
+    for o in range(1, SPAN + 1):
+
+        @pl.when(me >= o)
+        def _():
+            seg_copy(o).wait_recv()
+
+        @pl.when(me < o)
+        def _():
+            segs[o] = jnp.full((1, rows), -1, jnp.int32)
+
     hits = jnp.zeros_like(seg_row, jnp.float32)
     for o in range(1, SPAN + 1):
         hits += jnp.where(segs[o] == seg_first, 1.0, 0.0)
@@ -218,9 +312,9 @@
     per_pair = kv_heads * per_chunk
     steps = (SPAN + 1) // 2 * per_pair
 
-    def prepare(pair):
-        for part in range(2):
-            offset = 2 * pair + part
+    def prepare(pair, slots):
+        for part, slot in enumerate(slots):
+            offset = slot - 1 + core
             distance = (offset * rows).astype(jnp.float32)
             angle = (before - distance) * freq_row
             c, s = jnp.cos(angle), jnp.sin(angle)
@@ -250,29 +344,65 @@
     def chunk(q):
         pair, h = q // kv_heads, lax.rem(q, kv_heads)
         buf = lax.rem(q, 2)
+        forward = h < TURNED
+        back = h >= TURNED
+        far = REACH - pair
+
         ahead = 2 * pair + 3 - core
-
-        @pl.when(pair < REACH - 1)
-        def _():
-            hop(ahead - 2, pair, h).wait_recv()
-            side(ahead, pair + 1, h).start()
-
-        @pl.when(pair < REACH - 2)
-        def _():
-            hop(ahead, pair + 1, h).start()
-
-        @pl.when((pair == REACH - 2) & (core == 1))
+        mine = (pair < REACH - 1) & (chip >= pair + 1) & ((core == 0) | forward)
+
+        @pl.when(mine)
+        def _():
+            hop(ahead - 2, h).wait_recv()
+            side(ahead, h).start()
+
+        @pl.when(mine & (chip < last) & (pair < REACH - 2))
+        def _():
+            hop(ahead, h).start()
+
+        @pl.when(mine & (chip < last) & (pair == REACH - 2) & (core == 1))
         def _():
             last_hop(ahead, h).start()
 
-        @pl.when(h == 0)
-        def _():
-            prepare(pair)
-
-        unpack(2 * pair + 1 - core, h, 0, buf)
-        other = 2 * pair + 2 - core
-        side(other, 0, h).wait_recv()
-        unpack(other, h, 1, buf)
+        @pl.when(back & (pair == 0) & (core == 1) & (relayed < last))
+        def _():
+            first_leg(h).wait_recv()
+            second_leg(h).start()
+
+        chained = back & (core == 0) & (chip >= far)
+
+        @pl.when(chained)
+        def _():
+            side(2 * far, h).wait_recv()
+
+        @pl.when(chained & (far >= 2))
+        def _():
+            back_hop(2 * far, h).start()
+
+        @pl.when(chained & (far < REACH))
+        def _():
+            side(2 * far, h).start()
+
+        one = jnp.where(forward | (pair == 0), 2 * pair + 1 - core, 2 * pair + 1)
+        two = jnp.where(
+            forward, 2 * pair + 2 - core, jnp.where((pair == 0) & (core == 1), 1, 2 * far)
+        )
+
+        @pl.when((h == 0) | (h == TURNED))
+        def _():
+            prepare(pair, (one, two))
+
+        @pl.when(back & (pair > 0) & (core == 1) & (chip >= pair))
+        def _():
+            side(one, h).wait_recv()
+
+        unpack(one, h, 0, buf)
+
+        @pl.when((chip >= two // 2) & (forward | (core == 1)))
+        def _():
+            side(two, h).wait_recv()
+
+        unpack(two, h, 1, buf)
 
     def score(s, own):
         buf = lax.rem(s // per_chunk, 2)
@@ -367,22 +497,31 @@
         mix(jnp.int32(steps - 1))
         finish(h)
 
-    for copy in seg_copies:
-        copy.wait_send()
+    def drain(copy, when):
+        @pl.when(when)
+        def _():
+            copy.wait_send()
+
+    for o in range(1, SPAN + 1):
+        drain(seg_copy(o), me + o < n)
     for h in range(kv_heads):
-        for j in range(REACH - 1):
-            hop(0, j, h).wait_send()
-        for j in range(1, REACH):
-            side(0, j, h).wait_send()
-
-        @pl.when(core == 0)
-        def _():
-            side(0, 0, h).wait_send()
-
-        @pl.when(core == 1)
-        def _():
-            last_hop(0, h).wait_send()
-
+        lane_here = (core == 0) | (h < TURNED)
+        for j in range(REACH):
+            slot = 2 * j + own_slot
+            sends = lane_here & (chip >= j) & (chip < last)
+            if j == REACH - 1:
+                sends = sends & (core == 1)
+            drain(hop(slot, h), sends)
+            drain(side(slot, h), (lane_here & (chip >= j)) if j else core == 0)
+        if h >= TURNED:
+            drain(first_leg(h), (core == 1) & (chip < last))
+            drain(second_leg(h), (core == 1) & (relayed < last))
+            for j in range(1, REACH + 1):
+                turned = (core == 0) & (chip >= j)
+                if j >= 2:
+                    drain(back_hop(2 * j, h), turned)
+                if j < REACH:
+                    drain(side(2 * j, h), turned)
         store(h).wait()
     rk_store.wait()
 
@@ -437,8 +576,13 @@
             dma((4 + 2 * kv_heads,)),
             dma((SPAN,)),
             dma((SPAN,)),
-            dma((REACH, kv_heads)),
-            dma((REACH, kv_heads)),
+            dma((slots, kv_heads)),
+            dma((slots, kv_heads)),
+            dma((slots, kv_heads)),
+            pltpu.VMEM((kv_heads - TURNED, 2, rows, HD), bf16),
+            dma((kv_heads - TURNED,)),
+            dma((kv_heads - TURNED,)),
+            dma((kv_heads - TURNED,)),
             dma((slots, kv_heads)),
             dma((kv_heads,)),
         ],

time: 76.8 us -> 76.3 us (level)
  the two profiles are of different devices: /device:TPU:513 before, /device:TPU:529 now
where the time goes in v3:
time: 76.3 us; the launch traced here: 76.1 us
  Pallas kernels  71.6 us (94%)
  local copies, waits for them, and re-layouts  3.88 us (5%)
    pallas_call x1, Pallas kernels, local(): pl.pallas_call(functools.partial(kernel, kv_heads, group), out_shape=(jax...  71.6 us
    unnamed x4, local copies, waits for them, and re-layouts  3.88 us

profile of v3, /device:TPU:529, one launch (start us, length us, event | category | flops | bytes accessed | tf_op | source)
XLA Modules:
  0.0 76.1 jit_solution(17348191872697812117)
XLA Ops:
  0.6 71.6 %shard_map.77 = (bf16[256,4096]{1,0:T(8,128)(2,1)}, bf16[256,512]{1,0:T(8,128)(2,1)}) custom-call(s32[1,256]{1,0:T(1,128)} %bitcast.1, bf16[256,4096]{1,0:T(8,128)(2,1)} %q_in.1, bf16[256,512]{1,0:T(8,128)(2,1)} %k_in.1, bf16[256,512]{1,0:T(8,128)(2,1)} %v_in.1, f32[2,256,128]{2,1,0:T(8,128)} %constant.4.clone.table_in, f32[1,128]{1,0:T(1,128)} %constant.5.clone.freq_in), custom_call_target="tpu_custom_call" | custom-call | tf_op jit(solution)/shard_map/pallas_call | solution.py:543
  72.3 0.0 copy-start
  72.3 3.2 %copy.10 = bf16[256,4096]{1,0:T(8,128)(2,1)} copy(bf16[256,4096]{1,0:T(8,128)(2,1)} %get-tuple-element.4) | data formatting | bytes 4194304
  75.4 0.0 copy-done
  75.4 0.7 copy.11
Async XLA Ops:
  72.3 3.2 %copy-start = (bf16[256,512]{1,0:T(8,128)(2,1)S(1)}, bf16[256,512]{1,0:T(8,128)(2,1)}, u32[]{:S(2)}) copy-start(bf16[256,512]{1,0:T(8,128)(2,1)} %get-tuple-element.5) | copy-start | bytes 786436

commit v4 on v3

--- a/solution.py
+++ b/solution.py
@@ -12,7 +12,7 @@
 HD = 128
 SPAN = 7
 REACH = 4
-WIDE = 2
+STRIP = 128
 TURNED = 2
 ROPE_BASE = 1000000.0
 SCALE = float(HD ** (-0.5) * np.log2(np.e))
@@ -41,22 +41,18 @@
     tables,
     freq,
     qt,
-    qaug,
     diag,
     own_cos,
     own_sin,
     blk_cos,
     blk_sin,
     kx,
-    kaug,
     vt,
     top,
-    total,
+    anchor,
     acc,
     raw,
     peaks,
-    rounded,
-    fades,
     ovm,
     rkvm,
     in_sem,
@@ -256,16 +252,9 @@
     local_angle = local_position * freq_row
     local_cos = jnp.cos(local_angle)
     local_sin = jnp.sin(local_angle)
-    aug_at = lax.broadcasted_iota(jnp.int32, (HD, rows), 0)
-    later_row = jnp.where(first_row, 0.0, -BIG)
-    qaug[...] = jnp.where(
-        aug_at == 0, -BIG, jnp.where(aug_at == 1, later_row, 0.0)
-    ).astype(jnp.bfloat16)
-
     def clear(t, carry):
         top[t] = jnp.full((1, rows), -4.0 * BIG, jnp.float32)
-        total[t] = jnp.zeros((8, rows), jnp.float32)
-        acc[t] = jnp.zeros((HD, rows), jnp.float32)
+        acc[t] = jnp.zeros(acc.shape[1:], jnp.float32)
         return carry
 
     lax.fori_loop(0, kv_heads * group, clear, 0)
@@ -291,9 +280,9 @@
     own_sin[...] = (local_sin * base_cos + local_cos * base_sin) * sign
 
     for h in range(kv_heads):
-        rkvm[:, h * HD : (h + 1) * HD] = rotate(
-            kv[own_slot, h, 0], own_cos[...], own_sin[...]
-        ).astype(jnp.bfloat16)
+        turned_keys = rotate(kv[own_slot, h, 0], own_cos[...], own_sin[...])
+        anchor[h] = turned_keys[:8]
+        rkvm[:, h * HD : (h + 1) * HD] = turned_keys.astype(jnp.bfloat16)
     rk_store = pltpu.make_async_copy(rkvm, rk_out, in_sem.at[0])
     rk_store.start()
 
@@ -307,18 +296,33 @@
 
     lax.fori_loop(0, kv_heads * group, turn, 0)
 
-    wide_rows = 2 * rows
-    per_chunk = group // WIDE
-    per_pair = kv_heads * per_chunk
-    steps = (SPAN + 1) // 2 * per_pair
-
-    def prepare(pair, slots):
+    chunks = (SPAN + 1) // 2 * kv_heads
+    allowed_row = jnp.where(first_row, 0.0, -BIG)
+
+    def split(q):
+        pair = q // kv_heads
+        h = lax.rem(q, kv_heads)
+        h = jnp.where(pair == REACH - 1, lax.rem(h + TURNED, kv_heads), h)
+        return pair, h
+
+    def slots_of(pair, h):
+        forward = h < TURNED
+        one = jnp.where(forward | (pair == 0), 2 * pair + 1 - core, 2 * pair + 1)
+        two = jnp.where(
+            forward,
+            2 * pair + 2 - core,
+            jnp.where((pair == 0) & (core == 1), 1, 2 * (REACH - pair)),
+        )
+        return one, two
+
+    def missing(slot):
+        return ((slot - 1 + core) * rows).astype(jnp.float32) - before
+
+    def prepare(slots):
         for part, slot in enumerate(slots):
-            offset = slot - 1 + core
-            distance = (offset * rows).astype(jnp.float32)
-            angle = (before - distance) * freq_row
+            own = slot == own_slot
+            angle = -missing(slot) * freq_row
             c, s = jnp.cos(angle), jnp.sin(angle)
-            own = offset == 0
 
             @pl.when(own)
             def _():
@@ -330,20 +334,24 @@
                 blk_cos[part] = tables[0] * c - tables[1] * s
                 blk_sin[part] = (tables[1] * c + tables[0] * s) * sign
 
-            earlier = jnp.where(own, 0.0, 1.0)
-            invalid = (sublane < distance - before) & (lane == 0)
-            kaug[part * rows : (part + 1) * rows] = jnp.where(
-                invalid, 1.0, jnp.where(lane == 1, earlier, 0.0)
-            ).astype(jnp.bfloat16)
-
-    def unpack(slot, h, part, buf):
-        span = slice(part * rows, (part + 1) * rows)
-        kx[buf, span] = rotate(kv[slot, h, 0], blk_cos[part], blk_sin[part]).astype(jnp.bfloat16)
-        vt[buf, :, span] = kv[slot, h, 1].T
-
-    def chunk(q):
-        pair, h = q // kv_heads, lax.rem(q, kv_heads)
-        buf = lax.rem(q, 2)
+    def load_keys(q):
+        pair, h = split(q)
+        for part, slot in enumerate(slots_of(pair, h)):
+            turned = rotate(kv[slot, h, 0], blk_cos[part], blk_sin[part])
+            turned = jnp.where(sublane < missing(slot), anchor[h][:1], turned)
+            kx[part * rows : (part + 1) * rows] = turned.astype(jnp.bfloat16)
+
+    def load_values(q):
+        pair, h = split(q)
+        at = lax.broadcasted_iota(jnp.int32, (vt.shape[0] - HD, rows), 1).astype(jnp.float32)
+        for part, slot in enumerate(slots_of(pair, h)):
+            span = slice(part * rows, (part + 1) * rows)
+            kept = jnp.where(sublane < missing(slot), 0.0, kv[slot, h, 1].astype(jnp.float32))
+            vt[:HD, span] = kept.astype(jnp.bfloat16).T
+            vt[HD:, span] = jnp.where(at < missing(slot), 0.0, 1.0).astype(jnp.bfloat16)
+
+    def receive(q):
+        pair, h = split(q)
         forward = h < TURNED
         back = h >= TURNED
         far = REACH - pair
@@ -383,67 +391,50 @@
         def _():
             side(2 * far, h).start()
 
-        one = jnp.where(forward | (pair == 0), 2 * pair + 1 - core, 2 * pair + 1)
-        two = jnp.where(
-            forward, 2 * pair + 2 - core, jnp.where((pair == 0) & (core == 1), 1, 2 * far)
-        )
+        one, two = slots_of(pair, h)
 
         @pl.when((h == 0) | (h == TURNED))
         def _():
-            prepare(pair, (one, two))
+            prepare((one, two))
 
         @pl.when(back & (pair > 0) & (core == 1) & (chip >= pair))
         def _():
             side(one, h).wait_recv()
 
-        unpack(one, h, 0, buf)
-
         @pl.when((chip >= two // 2) & (forward | (core == 1)))
         def _():
             side(two, h).wait_recv()
 
-        unpack(two, h, 1, buf)
-
-    def score(s, own):
-        buf = lax.rem(s // per_chunk, 2)
-        for u in range(WIDE):
-            t = lax.rem(s, per_pair) * WIDE + u
-            scores = jnp.dot(
-                jnp.concatenate([kx[buf], kaug[...]], axis=1),
-                jnp.concatenate([qt[t], qaug[...]], axis=0),
-                preferred_element_type=jnp.float32,
-            )
-            low, high = scores[:rows], scores[rows:]
+    def score(q, u, own):
+        _, h = split(q)
+        t = h * group + u
+        peak = None
+        for at in range(0, 2 * rows, STRIP):
+            scores = jnp.dot(kx[at : at + STRIP], qt[t], preferred_element_type=jnp.float32)
             if own:
-                low = low + diag[...]
-            raw[u, :rows] = low
-            raw[u, rows:] = high
-            peaks[u] = jnp.maximum(
-                jnp.max(low.reshape(rows // 8, 8, rows), axis=0),
-                jnp.max(high.reshape(rows // 8, 8, rows), axis=0),
-            )
-
-    def weigh(s):
-        for u in range(WIDE):
-            t = lax.rem(s, per_pair) * WIDE + u
-            old = top[t]
-            peak = jnp.maximum(old, jnp.max(peaks[u], axis=0, keepdims=True))
-            fade = jnp.exp2((old - peak) * SCALE)
-            weights = jnp.exp2(raw[u] * SCALE - peak * SCALE)
-            top[t] = peak
-            total[t] = total[t] * fade + jnp.sum(
-                weights.reshape(wide_rows // 8, 8, rows), axis=0
-            )
-            rounded[u] = weights.astype(jnp.bfloat16)
-            fades[u] = fade
-
-    def mix(s):
-        buf = lax.rem(s // per_chunk, 2)
-        for u in range(WIDE):
-            t = lax.rem(s, per_pair) * WIDE + u
-            acc[t] = acc[t] * fades[u] + jnp.dot(
-                vt[buf], rounded[u], preferred_element_type=jnp.float32
-            )
+                scores += diag[at : at + STRIP] if at < rows else allowed_row
+            raw[u, at : at + STRIP] = scores
+            top_here = jnp.max(scores.reshape(STRIP // 8, 8, rows), axis=0)
+            peak = top_here if peak is None else jnp.maximum(peak, top_here)
+        peaks[u] = peak if own else jnp.where(first_row, peak, -BIG)
+
+    def weigh(q, u):
+        pair, h = split(q)
+        t = h * group + u
+        old = top[t]
+        peak = jnp.maximum(old, jnp.max(peaks[u], axis=0, keepdims=True))
+        fade = jnp.exp2((old - peak) * SCALE)
+        shift = jnp.where(first_row | (pair == 0), peak * SCALE, BIG)
+        shift = jnp.broadcast_to(shift, (8, rows))
+        top[t] = peak
+        weights = []
+        for at in range(0, 2 * rows, STRIP):
+            scores = raw[u, at : at + STRIP].reshape(STRIP // 8, 8, rows)
+            part = jnp.exp2(scores * SCALE - shift[None])
+            weights.append(part.reshape(STRIP, rows).astype(jnp.bfloat16))
+        acc[t] = acc[t] * fade + jnp.dot(
+            vt[...], jnp.concatenate(weights, axis=0), preferred_element_type=jnp.float32
+        )
 
     def store(h):
         at = pl.multiple_of(h * group * HD, group * HD)
@@ -451,51 +442,49 @@
             ovm.at[h], out.at[:, pl.ds(at, group * HD)], out_sem.at[h]
         )
 
-    def finish(h):
+    def finish(q):
+        _, h = split(q)
         for g in range(group):
             t = h * group + g
-            share = 1.0 / jnp.sum(total[t], axis=0, keepdims=True)
-            ovm[h, :, g * HD : (g + 1) * HD] = (acc[t] * share).astype(jnp.bfloat16).T
+            share = 1.0 / acc[t, HD : HD + 1]
+            ovm[h, :, g * HD : (g + 1) * HD] = (acc[t, :HD] * share).astype(jnp.bfloat16).T
         store(h).start()
 
-    def step(s, own):
-        @pl.when(lax.rem(s, per_chunk) == 0)
-        def _():
-            chunk(s // per_chunk)
-
-        mix(s - 2)
-        weigh(s - 1)
-        score(s, own)
-
-    chunk(jnp.int32(0))
-    score(jnp.int32(0), True)
-    if per_chunk == 1:
-        chunk(jnp.int32(1))
-    weigh(jnp.int32(0))
-    score(jnp.int32(1), True)
-
-    def own_step(s, carry):
-        step(s, True)
+    def step(q, own):
+        receive(q)
+        load_keys(q)
+        load_values(q - 1)
+        for u in range(group):
+            weigh(q - 1, u)
+            score(q, u, own)
+
+    first = jnp.int32(0)
+    receive(first)
+    load_keys(first)
+    for u in range(group):
+        score(first, u, True)
+
+    def own_step(q, carry):
+        step(q, True)
         return carry
 
-    lax.fori_loop(2, per_pair, own_step, 0)
-
-    def later_step(s, carry):
-        ready = s - 2 - (steps - per_pair)
-
-        @pl.when((ready > 0) & (lax.rem(ready, per_chunk) == 0))
-        def _():
-            finish(ready // per_chunk - 1)
-
-        step(s, False)
+    lax.fori_loop(1, kv_heads, own_step, 0)
+
+    def later_step(q, carry):
+        @pl.when(q >= chunks - kv_heads + 2)
+        def _():
+            finish(q - 2)
+
+        step(q, False)
         return carry
 
-    lax.fori_loop(per_pair, steps, later_step, 0)
-    mix(jnp.int32(steps - 2))
-    weigh(jnp.int32(steps - 1))
-    for h in range(kv_heads - 1, kv_heads):
-        mix(jnp.int32(steps - 1))
-        finish(h)
+    lax.fori_loop(kv_heads, chunks, later_step, 0)
+    final = jnp.int32(chunks - 1)
+    load_values(final)
+    finish(final - 1)
+    for u in range(group):
+        weigh(final, u)
+    finish(final)
 
     def drain(copy, when):
         @pl.when(when)
@@ -555,22 +544,18 @@
             pltpu.VMEM((2, rows, HD), f32),
             pltpu.VMEM((1, HD), f32),
             pltpu.VMEM((heads, HD, rows), bf16),
-            pltpu.VMEM((HD, rows), bf16),
             pltpu.VMEM((rows, rows), f32),
             pltpu.VMEM((rows, HD), f32),
             pltpu.VMEM((rows, HD), f32),
             pltpu.VMEM((2, rows, HD), f32),
             pltpu.VMEM((2, rows, HD), f32),
-            pltpu.VMEM((2, 2 * rows, HD), bf16),
             pltpu.VMEM((2 * rows, HD), bf16),
-            pltpu.VMEM((2, HD, 2 * rows), bf16),
+            pltpu.VMEM((HD + 16, 2 * rows), bf16),
             pltpu.VMEM((heads, 1, rows), f32),
-            pltpu.VMEM((heads, 8, rows), f32),
-            pltpu.VMEM((heads, HD, rows), f32),
-            pltpu.VMEM((WIDE, 2 * rows, rows), f32),
-            pltpu.VMEM((WIDE, 8, rows), f32),
-            pltpu.VMEM((WIDE, 2 * rows, rows), bf16),
-            pltpu.VMEM((WIDE, 1, rows), f32),
+            pltpu.VMEM((kv_heads, 8, HD), f32),
+            pltpu.VMEM((heads, HD + 16, rows), f32),
+            pltpu.VMEM((group, 2 * rows, rows), f32),
+            pltpu.VMEM((group, 8, rows), f32),
             pltpu.VMEM((kv_heads, rows, group * HD), bf16),
             pltpu.VMEM((rows, kv_width), bf16),
             dma((4 + 2 * kv_heads,)),

time: 76.3 us -> 69.3 us (0.908)
  the two profiles are of different devices: /device:TPU:529 before, /device:TPU:527 now
where the time goes in v4:
time: 69.3 us; the launch traced here: 69.1 us
  Pallas kernels  64.6 us (93%)
  local copies, waits for them, and re-layouts  3.88 us (6%)
    pallas_call x1, Pallas kernels, local(): pl.pallas_call(functools.partial(kernel, kv_heads, group), out_shape=(jax...  64.6 us
    unnamed x4, local copies, waits for them, and re-layouts  3.88 us

profile of v4, /device:TPU:527, one launch (start us, length us, event | category | flops | bytes accessed | tf_op | source)
XLA Modules:
  0.0 69.1 jit_solution(14082249404818379089)
XLA Ops:
  0.6 64.6 %shard_map.77 = (bf16[256,4096]{1,0:T(8,128)(2,1)}, bf16[256,512]{1,0:T(8,128)(2,1)}) custom-call(s32[1,256]{1,0:T(1,128)} %bitcast.1, bf16[256,4096]{1,0:T(8,128)(2,1)} %q_in.1, bf16[256,512]{1,0:T(8,128)(2,1)} %k_in.1, bf16[256,512]{1,0:T(8,128)(2,1)} %v_in.1, f32[2,256,128]{2,1,0:T(8,128)} %constant.4.clone.table_in, f32[1,128]{1,0:T(1,128)} %constant.5.clone.freq_in), custom_call_target="tpu_custom_call" | custom-call | tf_op jit(solution)/shard_map/pallas_call | solution.py:532
  65.2 0.0 copy-start
  65.2 3.2 %copy.10 = bf16[256,4096]{1,0:T(8,128)(2,1)} copy(bf16[256,4096]{1,0:T(8,128)(2,1)} %get-tuple-element.4) | data formatting | bytes 4194304
  68.4 0.0 copy-done
  68.4 0.7 %copy.11 = bf16[256,512]{1,0:T(8,128)(2,1)} copy(bf16[256,512]{1,0:T(8,128)(2,1)S(1)} %copy-done) | data formatting | bytes 524288
Async XLA Ops:
  65.2 3.2 %copy-start = (bf16[256,512]{1,0:T(8,128)(2,1)S(1)}, bf16[256,512]{1,0:T(8,128)(2,1)}, u32[]{:S(2)}) copy-start(bf16[256,512]{1,0:T(8,128)(2,1)} %get-tuple-element.5) | copy-start | bytes 786436

commit v5 on v4

--- a/solution.py
+++ b/solution.py
@@ -230,6 +230,35 @@
 
     lax.fori_loop(2, 2 * REACH + 1, blank, 0)
 
+    def relay(j, h, early):
+        ahead = 2 * j + 1 - core
+        before_ids = (chip < REACH) & (j < chip)
+        mine = (j < REACH) & (chip >= j) & ((core == 0) | (h < TURNED))
+        mine = mine & (before_ids if early else jnp.logical_not(before_ids))
+
+        @pl.when(mine)
+        def _():
+            hop(ahead - 2, h).wait_recv()
+            side(ahead, h).start()
+
+        @pl.when(mine & (chip < last) & (j < REACH - 1))
+        def _():
+            hop(ahead, h).start()
+
+        @pl.when(mine & (chip < last) & (j == REACH - 1) & (core == 1))
+        def _():
+            last_hop(ahead, h).start()
+
+    def turn_back(early):
+        when = (core == 1) & (relayed < last)
+        when = when & ((chip < REACH) if early else (chip >= REACH))
+
+        @pl.when(when)
+        def _():
+            for h in range(TURNED, kv_heads):
+                first_leg(h).wait_recv()
+                second_leg(h).start()
+
     freq_load.wait()
     table_load.wait()
     lane = lax.broadcasted_iota(jnp.int32, (rows, HD), 1)
@@ -259,6 +288,14 @@
 
     lax.fori_loop(0, kv_heads * group, clear, 0)
 
+    turn_back(True)
+
+    def early_relay(i, carry):
+        relay(i // kv_heads, lax.rem(i, kv_heads), True)
+        return carry
+
+    lax.fori_loop(kv_heads, (REACH - 1) * kv_heads, early_relay, 0)
+
     for o in range(1, SPAN + 1):
 
         @pl.when(me >= o)
@@ -295,14 +332,19 @@
         return carry
 
     lax.fori_loop(0, kv_heads * group, turn, 0)
+    turn_back(False)
 
     chunks = (SPAN + 1) // 2 * kv_heads
     allowed_row = jnp.where(first_row, 0.0, -BIG)
 
     def split(q):
-        pair = q // kv_heads
-        h = lax.rem(q, kv_heads)
-        h = jnp.where(pair == REACH - 1, lax.rem(h + TURNED, kv_heads), h)
+        part, i = q // kv_heads, lax.rem(q, kv_heads)
+        pair = jnp.where(part < 2, i // TURNED, part)
+        h = jnp.where(
+            part < 2,
+            lax.rem(i, TURNED) + TURNED * part,
+            jnp.where(part == REACH - 1, lax.rem(i + TURNED, kv_heads), i),
+        )
         return pair, h
 
     def slots_of(pair, h):
@@ -356,26 +398,18 @@
         back = h >= TURNED
         far = REACH - pair
 
-        ahead = 2 * pair + 3 - core
-        mine = (pair < REACH - 1) & (chip >= pair + 1) & ((core == 0) | forward)
-
-        @pl.when(mine)
-        def _():
-            hop(ahead - 2, h).wait_recv()
-            side(ahead, h).start()
-
-        @pl.when(mine & (chip < last) & (pair < REACH - 2))
-        def _():
-            hop(ahead, h).start()
-
-        @pl.when(mine & (chip < last) & (pair == REACH - 2) & (core == 1))
-        def _():
-            last_hop(ahead, h).start()
-
-        @pl.when(back & (pair == 0) & (core == 1) & (relayed < last))
-        def _():
-            first_leg(h).wait_recv()
-            second_leg(h).start()
+        @pl.when(forward & (pair == 1))
+        def _():
+            @pl.when(h == 0)
+            def _():
+                for g in range(TURNED, kv_heads):
+                    relay(1, g, False)
+
+        turn_ahead = jnp.where(forward | (pair >= 2), pair + 1, 2)
+
+        @pl.when(forward | (pair != 1))
+        def _():
+            relay(turn_ahead, h, False)
 
         chained = back & (core == 0) & (chip >= far)
 
@@ -464,21 +498,24 @@
     for u in range(group):
         score(first, u, True)
 
-    def own_step(q, carry):
-        step(q, True)
+    def every_step(q, carry):
+        @pl.when(q >= chunks - kv_heads + 2)
+        def _():
+            finish(q - 2)
+
+        pair, _ = split(q)
+
+        @pl.when(pair == 0)
+        def _():
+            step(q, True)
+
+        @pl.when(pair > 0)
+        def _():
+            step(q, False)
+
         return carry
 
-    lax.fori_loop(1, kv_heads, own_step, 0)
-
-    def later_step(q, carry):
-        @pl.when(q >= chunks - kv_heads + 2)
-        def _():
-            finish(q - 2)
-
-        step(q, False)
-        return carry
-
-    lax.fori_loop(kv_heads, chunks, later_step, 0)
+    lax.fori_loop(1, chunks, every_step, 0)
     final = jnp.int32(chunks - 1)
     load_values(final)
     finish(final - 1)

time: 69.3 us -> 65.5 us (0.945)
  the two profiles are of different devices: /device:TPU:527 before, /device:TPU:645 now
where the time goes in v5:
time: 65.5 us; the launch traced here: 65.3 us
  Pallas kernels  60.8 us (93%)
  local copies, waits for them, and re-layouts  3.88 us (6%)
    pallas_call x1, Pallas kernels, local(): pl.pallas_call(functools.partial(kernel, kv_heads, group), out_shape=(jax...  60.8 us
    unnamed x4, local copies, waits for them, and re-layouts  3.88 us

profile of v5, /device:TPU:645, one launch (start us, length us, event | category | flops | bytes accessed | tf_op | source)
XLA Modules:
  0.0 65.3 jit_solution(8542673210794719674)
XLA Ops:
  0.6 60.8 %shard_map.77 = (bf16[256,4096]{1,0:T(8,128)(2,1)}, bf16[256,512]{1,0:T(8,128)(2,1)}) custom-call(s32[1,256]{1,0:T(1,128)} %bitcast.1, bf16[256,4096]{1,0:T(8,128)(2,1)} %q_in.1, bf16[256,512]{1,0:T(8,128)(2,1)} %k_in.1, bf16[256,512]{1,0:T(8,128)(2,1)} %v_in.1, f32[2,256,128]{2,1,0:T(8,128)} %constant.4.clone.table_in, f32[1,128]{1,0:T(1,128)} %constant.5.clone.freq_in), custom_call_target="tpu_custom_call" | custom-call | tf_op jit(solution)/shard_map/pallas_call | solution.py:569
  61.4 0.0 copy-start
  61.4 3.2 %copy.10 = bf16[256,4096]{1,0:T(8,128)(2,1)} copy(bf16[256,4096]{1,0:T(8,128)(2,1)} %get-tuple-element.4) | data formatting | bytes 4194304
  64.6 0.0 copy-done
  64.6 0.7 %copy.11 = bf16[256,512]{1,0:T(8,128)(2,1)} copy(bf16[256,512]{1,0:T(8,128)(2,1)S(1)} %copy-done) | data formatting | bytes 524288
Async XLA Ops:
  61.4 3.2 %copy-start = (bf16[256,512]{1,0:T(8,128)(2,1)S(1)}, bf16[256,512]{1,0:T(8,128)(2,1)}, u32[]{:S(2)}) copy-start(bf16[256,512]{1,0:T(8,128)(2,1)} %get-tuple-element.5) | copy-start | bytes 786436

commit v6 on v5

--- a/solution.py
+++ b/solution.py
@@ -53,8 +53,6 @@
     acc,
     raw,
     peaks,
-    ovm,
-    rkvm,
     in_sem,
     seg_send,
     seg_recv,
@@ -66,7 +64,6 @@
     via_recv,
     leg_send,
     kv_recv,
-    out_sem,
 ):
     rows = q_in.shape[0]
     half = HD // 2
@@ -319,9 +316,7 @@
     for h in range(kv_heads):
         turned_keys = rotate(kv[own_slot, h, 0], own_cos[...], own_sin[...])
         anchor[h] = turned_keys[:8]
-        rkvm[:, h * HD : (h + 1) * HD] = turned_keys.astype(jnp.bfloat16)
-    rk_store = pltpu.make_async_copy(rkvm, rk_out, in_sem.at[0])
-    rk_store.start()
+        rk_out[:, h * HD : (h + 1) * HD] = turned_keys.astype(jnp.bfloat16)
 
     q_load.wait()
 
@@ -470,19 +465,13 @@
             vt[...], jnp.concatenate(weights, axis=0), preferred_element_type=jnp.float32
         )
 
-    def store(h):
-        at = pl.multiple_of(h * group * HD, group * HD)
-        return pltpu.make_async_copy(
-            ovm.at[h], out.at[:, pl.ds(at, group * HD)], out_sem.at[h]
-        )
-
     def finish(q):
         _, h = split(q)
         for g in range(group):
             t = h * group + g
             share = 1.0 / acc[t, HD : HD + 1]
-            ovm[h, :, g * HD : (g + 1) * HD] = (acc[t, :HD] * share).astype(jnp.bfloat16).T
-        store(h).start()
+            at = pl.multiple_of(t * HD, HD)
+            out[:, pl.ds(at, HD)] = (acc[t, :HD] * share).astype(jnp.bfloat16).T
 
     def step(q, own):
         receive(q)
@@ -548,8 +537,6 @@
                     drain(back_hop(2 * j, h), turned)
                 if j < REACH:
                     drain(side(2 * j, h), turned)
-        store(h).wait()
-    rk_store.wait()
 
 
 def local(queries, keys, values, segment_ids):
@@ -562,18 +549,18 @@
     freq = np.concatenate([freq, freq])[None]
     angle = (np.arange(rows, dtype=np.float32)[:, None] * freq).astype(np.float64)
     table = np.stack([np.cos(angle), np.sin(angle)]).astype(np.float32)
-    any_space = pl.BlockSpec(memory_space=pl.ANY)
+    in_hbm = pl.BlockSpec(memory_space=pltpu.HBM)
     bf16, f32 = jnp.bfloat16, jnp.float32
     slots = 2 * REACH + 1
     dma = pltpu.SemaphoreType.DMA
     return pl.pallas_call(
         functools.partial(kernel, kv_heads, group),
         out_shape=(
-            jax.ShapeDtypeStruct((rows, width), bf16),
-            jax.ShapeDtypeStruct((rows, kv_width), bf16),
+            pltpu.VMEM((rows, width), bf16),
+            pltpu.VMEM((rows, kv_width), bf16),
         ),
-        in_specs=[any_space] * 6,
-        out_specs=(any_space, any_space),
+        in_specs=[in_hbm] * 6,
+        out_specs=(pl.BlockSpec(memory_space=pltpu.VMEM),) * 2,
         scratch_shapes=[
             pltpu.VMEM((SPAN + 1, 1, rows), jnp.int32),
             pltpu.VMEM((rows, width), bf16),
@@ -593,8 +580,6 @@
             pltpu.VMEM((heads, HD + 16, rows), f32),
             pltpu.VMEM((group, 2 * rows, rows), f32),
             pltpu.VMEM((group, 8, rows), f32),
-            pltpu.VMEM((kv_heads, rows, group * HD), bf16),
-            pltpu.VMEM((rows, kv_width), bf16),
             dma((4 + 2 * kv_heads,)),
             dma((SPAN,)),
             dma((SPAN,)),
@@ -606,10 +591,9 @@
             dma((kv_heads - TURNED,)),
             dma((kv_heads - TURNED,)),
             dma((slots, kv_heads)),
-            dma((kv_heads,)),
         ],
         compiler_params=pltpu.CompilerParams(
-            collective_id=0, has_side_effects=True, vmem_limit_bytes=56 * 1024 * 1024
+            collective_id=0, has_side_effects=True, vmem_limit_bytes=64500000
         ),
     )(
         segment_ids.reshape(1, rows),

time: 65.5 us -> 62.8 us (0.959)
  local copies, waits for them, and re-layouts: 3.88 us -> 2.02 us
  Pallas kernels: 60.8 us -> 60.1 us
    unnamed x4 -> x2, local copies, waits for them, and re-layouts: 3.88 us -> 2.02 us
    pallas_call x1, Pallas kernels: 60.8 us -> 60.1 us  [local(): pl.pallas_call(functools.partial(kernel, kv_heads, group), out_shape=(plt...]
where the time goes in v6:
time: 62.8 us; the launch traced here: 62.7 us
  Pallas kernels  60.1 us (96%)
  local copies, waits for them, and re-layouts  2.02 us (3%)
  between operations  0.64 us (1%)
    pallas_call x1, Pallas kernels, local(): pl.pallas_call(functools.partial(kernel, kv_heads, group), out_shape=(plt...  60.1 us
    unnamed x2, local copies, waits for them, and re-layouts  2.02 us

profile of v6, /device:TPU:645, one launch (start us, length us, event | category | flops | bytes accessed | tf_op | source)
XLA Modules:
  0.0 62.7 jit_solution(6010803000014443335)
XLA Ops:
  0.6 60.1 %shard_map.77 = (bf16[256,4096]{1,0:T(8,128)(2,1)S(1)}, bf16[256,512]{1,0:T(8,128)(2,1)S(1)}) custom-call(s32[1,256]{1,0:T(1,128)} %bitcast.1, bf16[256,4096]{1,0:T(8,128)(2,1)} %q_in.1, bf16[256,512]{1,0:T(8,128)(2,1)} %k_in.1, bf16[256,512]{1,0:T(8,128)(2,1)} %v_in.1, f32[2,256,128]{2,1,0:T(8,128)} %constant.4.clone.table_in, f32[1,128]{1,0:T(1,128)} %constant.5.clone.freq_in), custom_call_target="tpu_custom_call" | custom-call | tf_op jit(solution)/shard_map/pallas_call | solution.py:556
  60.7 1.3 %copy.10 = bf16[256,4096]{1,0:T(8,128)(2,1)} copy(bf16[256,4096]{1,0:T(8,128)(2,1)S(1)} %get-tuple-element.2) | data formatting | bytes 4194304
  62.0 0.7 %copy.11 = bf16[256,512]{1,0:T(8,128)(2,1)} copy(bf16[256,512]{1,0:T(8,128)(2,1)S(1)} %get-tuple-element.3) | data formatting | bytes 524288

commit v7 on v6

--- a/solution.py
+++ b/solution.py
@@ -114,15 +114,16 @@
     for o in range(1, SPAN + 1):
         tell(me - o, me >= o)
     tell(me + 1, (core == 0) & (chip >= 1))
-    tell(me + 2, (core == 0) & (chip >= 1) & (chip < last))
+    tell(me + 2, (core == 1) & (chip >= 1) & (chip < last))
     tell(2 * relayed + 1, (core == 1) & (relayed < last))
-    tell(2 * relay_of(chip - REACH) + 1, (core == 0) & (chip >= REACH))
+    tell(2 * relay_of(chip - REACH) + 1, (core == 1) & (chip >= REACH))
     for back in range(1, REACH):
-        tell(2 * relay_of(chip - back) + 1, (core == 0) & (chip == last))
+        tell(2 * relay_of(chip - back) + 1, (core == 1) & (chip == last))
     receivers = jnp.minimum(SPAN, n - 1 - me) + jnp.where(
         core == 0,
-        jnp.where(chip >= 2, 1, 0),
+        0,
         jnp.where(chip >= 1, 1, 0)
+        + jnp.where(chip >= 2, 1, 0)
         + jnp.where(chip < last, 1, 0)
         + jnp.where(relayed < last, 1, 0),
     )
@@ -197,7 +198,7 @@
             dst_ref=kv.at[slot, h],
             send_sem=leg_send.at[h - TURNED],
             recv_sem=kv_recv.at[slot, h],
-            device_id={"seq": 2 * far},
+            device_id={"seq": 2 * far + 1},
         )
 
     for h in range(kv_heads):
@@ -406,18 +407,16 @@
         def _():
             relay(turn_ahead, h, False)
 
-        chained = back & (core == 0) & (chip >= far)
+        chained = back & (core == 1) & (chip >= far)
 
         @pl.when(chained)
         def _():
             side(2 * far, h).wait_recv()
 
-        @pl.when(chained & (far >= 2))
-        def _():
-            back_hop(2 * far, h).start()
-
-        @pl.when(chained & (far < REACH))
-        def _():
+            @pl.when(far >= 2)
+            def _():
+                back_hop(2 * far, h).start()
+
             side(2 * far, h).start()
 
         one, two = slots_of(pair, h)
@@ -430,7 +429,7 @@
         def _():
             side(one, h).wait_recv()
 
-        @pl.when((chip >= two // 2) & (forward | (core == 1)))
+        @pl.when((chip >= two // 2) & (forward | (core == 0) | (pair == 0)))
         def _():
             side(two, h).wait_recv()
 
@@ -532,11 +531,10 @@
             drain(first_leg(h), (core == 1) & (chip < last))
             drain(second_leg(h), (core == 1) & (relayed < last))
             for j in range(1, REACH + 1):
-                turned = (core == 0) & (chip >= j)
+                turned = (core == 1) & (chip >= j)
                 if j >= 2:
                     drain(back_hop(2 * j, h), turned)
-                if j < REACH:
-                    drain(side(2 * j, h), turned)
+                drain(side(2 * j, h), turned)
 
 
 def local(queries, keys, values, segment_ids):

time: 62.8 us -> 59.2 us (0.943)
  the two profiles are of different devices: /device:TPU:645 before, /device:TPU:514 now
where the time goes in v7:
time: 59.2 us; the launch traced here: 59.1 us
  Pallas kernels  56.4 us (95%)
  local copies, waits for them, and re-layouts  2.02 us (3%)
  between operations  0.64 us (1%)
    pallas_call x1, Pallas kernels, local(): pl.pallas_call(functools.partial(kernel, kv_heads, group), out_shape=(plt...  56.4 us
    unnamed x2, local copies, waits for them, and re-layouts  2.02 us

profile of v7, /device:TPU:514, one launch (start us, length us, event | category | flops | bytes accessed | tf_op | source)
XLA Modules:
  0.0 59.1 jit_solution(5692834478703004453)
XLA Ops:
  0.6 56.4 %shard_map.77 = (bf16[256,4096]{1,0:T(8,128)(2,1)S(1)}, bf16[256,512]{1,0:T(8,128)(2,1)S(1)}) custom-call(s32[1,256]{1,0:T(1,128)} %bitcast.1, bf16[256,4096]{1,0:T(8,128)(2,1)} %q_in.1, bf16[256,512]{1,0:T(8,128)(2,1)} %k_in.1, bf16[256,512]{1,0:T(8,128)(2,1)} %v_in.1, f32[2,256,128]{2,1,0:T(8,128)} %constant.4.clone.table_in, f32[1,128]{1,0:T(1,128)} %constant.5.clone.freq_in), custom_call_target="tpu_custom_call" | custom-call | tf_op jit(solution)/shard_map/pallas_call | solution.py:554
  57.0 1.3 %copy.10 = bf16[256,4096]{1,0:T(8,128)(2,1)} copy(bf16[256,4096]{1,0:T(8,128)(2,1)S(1)} %get-tuple-element.2) | data formatting | bytes 4194304
  58.4 0.7 %copy.11 = bf16[256,512]{1,0:T(8,128)(2,1)} copy(bf16[256,512]{1,0:T(8,128)(2,1)S(1)} %get-tuple-element.3) | data formatting | bytes 524288

commit v8 on v7

--- a/solution.py
+++ b/solution.py
@@ -327,7 +327,7 @@
         qt[t] = turned.astype(jnp.bfloat16).T
         return carry
 
-    lax.fori_loop(0, kv_heads * group, turn, 0)
+    lax.fori_loop(0, kv_heads * group, turn, 0, unroll=4)
     turn_back(False)
 
     chunks = (SPAN + 1) // 2 * kv_heads
@@ -472,12 +472,17 @@
             at = pl.multiple_of(t * HD, HD)
             out[:, pl.ds(at, HD)] = (acc[t, :HD] * share).astype(jnp.bfloat16).T
 
-    def step(q, own):
-        receive(q)
+    short = chip < REACH - 1
+
+    def taken(q):
+        one, two = slots_of(*split(q))
+        return (chip >= one // 2) | (chip >= two // 2)
+
+    def step(q, held, own):
         load_keys(q)
-        load_values(q - 1)
+        load_values(held)
         for u in range(group):
-            weigh(q - 1, u)
+            weigh(held, u)
             score(q, u, own)
 
     first = jnp.int32(0)
@@ -486,29 +491,36 @@
     for u in range(group):
         score(first, u, True)
 
-    def every_step(q, carry):
-        @pl.when(q >= chunks - kv_heads + 2)
+    def every_step(q, held):
+        @pl.when((q >= chunks - kv_heads + 2) & jnp.logical_not(short))
         def _():
             finish(q - 2)
 
+        receive(q)
         pair, _ = split(q)
 
         @pl.when(pair == 0)
         def _():
-            step(q, True)
-
-        @pl.when(pair > 0)
-        def _():
-            step(q, False)
-
-        return carry
-
-    lax.fori_loop(1, chunks, every_step, 0)
+            step(q, held, True)
+
+        @pl.when((pair > 0) & taken(q))
+        def _():
+            step(q, held, False)
+
+        return jnp.where(taken(q), q, held)
+
+    held = lax.fori_loop(1, chunks, every_step, first)
     final = jnp.int32(chunks - 1)
-    load_values(final)
+    load_values(held)
     finish(final - 1)
     for u in range(group):
-        weigh(final, u)
+        weigh(held, u)
+
+    def finish_late(i, carry):
+        finish(final - i)
+        return carry
+
+    lax.fori_loop(2, jnp.where(short, kv_heads, 2), finish_late, 0)
     finish(final)
 
     def drain(copy, when):

time: 59.2 us -> 56.7 us (0.958)
  the two profiles are of different devices: /device:TPU:514 before, /device:TPU:646 now
where the time goes in v8:
time: 56.7 us; the launch traced here: 56.6 us
  Pallas kernels  53.9 us (95%)
  local copies, waits for them, and re-layouts  2.02 us (4%)
  between operations  0.64 us (1%)
    pallas_call x1, Pallas kernels, local(): pl.pallas_call(functools.partial(kernel, kv_heads, group), out_shape=(plt...  53.9 us
    unnamed x2, local copies, waits for them, and re-layouts  2.02 us

profile of v8, /device:TPU:646, one launch (start us, length us, event | category | flops | bytes accessed | tf_op | source)
XLA Modules:
  0.0 56.6 jit_solution(9275391826615780878)
XLA Ops:
  0.6 53.9 %shard_map.77 = (bf16[256,4096]{1,0:T(8,128)(2,1)S(1)}, bf16[256,512]{1,0:T(8,128)(2,1)S(1)}) custom-call(s32[1,256]{1,0:T(1,128)} %bitcast.1, bf16[256,4096]{1,0:T(8,128)(2,1)} %q_in.1, bf16[256,512]{1,0:T(8,128)(2,1)} %k_in.1, bf16[256,512]{1,0:T(8,128)(2,1)} %v_in.1, f32[2,256,128]{2,1,0:T(8,128)} %constant.4.clone.table_in, f32[1,128]{1,0:T(1,128)} %constant.5.clone.freq_in), custom_call_target="tpu_custom_call" | custom-call | tf_op jit(solution)/shard_map/pallas_call | solution.py:566
  54.5 1.3 %copy.10 = bf16[256,4096]{1,0:T(8,128)(2,1)} copy(bf16[256,4096]{1,0:T(8,128)(2,1)S(1)} %get-tuple-element.2) | data formatting | bytes 4194304
  55.9 0.7 %copy.11 = bf16[256,512]{1,0:T(8,128)(2,1)} copy(bf16[256,512]{1,0:T(8,128)(2,1)S(1)} %get-tuple-element.3) | data formatting | bytes 524288
